TPU v7x, 512 devices: a whole 4x4x16 slice. The times are simulated.
512 devices in a mesh: rows: 128 (over x, z, core), grp: 4 (over y).
Axes of the slice: x: 4, y: 4, z: 16, core: 2. Of those that a mesh axis runs over, the one named last changes fastest.
Arguments:
- operator: float32 [24576, 24576], P('rows', 'grp')
- block_inverse: float32 [3072, 24, 24], P('rows')
- block_len: int32 [128, 24], P('rows'), may hold values from 1 to 24, 192 in all within a row
- iterate: float32 [6, 24576], P(None, 'rows'), may hold values from -6 to 6
- residual: float32 [6, 24576], P(None, 'rows')
Outputs:
- new_iterate: float32 [6, 24576], P(None, 'rows')
- new_residual: float32 [6, 24576], P(None, 'rows')
Inputs may be any that keep to these rules, and one draw needn't show every extreme that they name: Each row of block_len sums to 192.
All inputs are finite; a program needn't handle non-finite values.
Results may differ from a plain program's by a relative error of at most 0.0003.
Values sent between devices are 32-bit elements; how exact they have to be, the bound alone decides.
No kernel may reach another device: no remote copies, remote signals or barrier semaphores. Data moves between devices by JAX's collectives and lax.ppermute only.
A program may use at most 64 MiB of HBM per device.

v0:
```python
import jax
import jax.numpy as jnp
from jax import lax
from jax.sharding import Mesh
from jax.sharding import PartitionSpec as P

ROWS = ("rows_0", "rows_1", "rows_2")


highest = lax.Precision.HIGHEST


def cut_along(array, dim, size):
    lengths = array.shape
    pieces = array.reshape(*lengths[:dim], size, lengths[dim] // size, *lengths[dim + 1 :])
    return jnp.moveaxis(pieces, dim, 0)


def summed_on_arrival(array, axis, dim):
    pieces = cut_along(array, dim, lax.axis_size(axis))
    arrived = lax.all_to_all(pieces, axis, split_axis=0, concat_axis=0, tiled=True)
    return arrived.sum(axis=0)


def summed_rows(array, axes, dim):
    far, near = axes
    pieces = cut_along(array, dim, lax.axis_size(far))
    nearer = summed_on_arrival(pieces, near, dim + 1)
    arrived = lax.all_to_all(nearer, far, split_axis=0, concat_axis=0, tiled=True)
    return arrived.sum(axis=0)


def filled_up(lines, size):
    spare = -len(lines) % size
    return jnp.pad(lines, [(0, spare)] + [(0, 0)] * (lines.ndim - 1))


def from_everyone(array, axis):
    copies = jnp.broadcast_to(array, (lax.axis_size(axis), *array.shape))
    return lax.all_to_all(copies, axis, split_axis=0, concat_axis=0, tiled=True)


def laid_out(pieces, dim):
    pieces = jnp.moveaxis(pieces, 0, dim)
    lengths = pieces.shape
    return pieces.reshape(*lengths[:dim], lengths[dim] * lengths[dim + 1], *lengths[dim + 2 :])


def gather_axes(array, axes, dim):
    far, near = axes
    leading = from_everyone(array, far)
    pieces = jnp.swapaxes(from_everyone(leading, near), 0, 1)
    return laid_out(pieces.reshape(-1, *array.shape), dim)


def sum_by_parts(array, axes):
    lines = array.reshape(-1)
    own = summed_rows(filled_up(lines, lax.axis_size(axes[0]) * lax.axis_size(axes[1])), axes, 0)
    whole = gather_axes(own, axes, 0)
    return whole[: len(lines)].reshape(array.shape)


def gathered_copies(array, axis, dim):
    return laid_out(from_everyone(array, axis), dim)


def taken_together(array, axis):
    everything = from_everyone(array, axis)
    return jnp.sum(everything, axis=0)


def by_axis(array, axes):
    far, near = axes
    nearer = taken_together(array, near)
    return taken_together(nearer, far)


def together(arrays, axis):
    ends = [0]
    for a in arrays:
        ends.append(ends[-1] + a.size)
    subtotal = by_axis(jnp.concatenate([a.ravel() for a in arrays]), axis)
    return tuple((subtotal[b:e].reshape(a.shape) for a, b, e in zip(arrays, ends, ends[1:])))


def block_apply(lengths, inverse, vector):
    width = vector.shape[1]
    depth = inverse.shape[1]
    starts = jnp.cumsum(lengths) - lengths
    offset = jnp.arange(depth, dtype=jnp.int32)
    column = jnp.arange(width, dtype=jnp.int32)
    select = (
        (column[None, None, :] == starts[:, None, None] + offset[None, :, None])
        & (offset[None, :, None] < lengths[:, None, None])
    ).astype(jnp.float32)
    pieces = jnp.einsum("bku,ru->rbk", select, vector, precision=highest)
    solved = jnp.einsum("bkl,rbl->rbk", inverse, pieces, precision=highest)
    return jnp.einsum("bku,rbk->ru", select, solved, precision=highest)


def dotted(first, second):
    return jnp.sum(first * second, axis=1)


def body(operator, block_inverse, block_len, iterate, residual):
    lengths = block_len[0]
    unknowns = iterate.shape[1]
    position = lax.axis_index(ROWS)

    def precondition(vector):
        return block_apply(lengths, block_inverse, vector)

    def product(vector):
        partial_value = jnp.dot(vector, operator, precision=highest)
        totals = sum_by_parts(partial_value, (("rows_0", "rows_1"), "rows_2"))
        gathered = gathered_copies(totals, "grp", 1)
        return lax.dynamic_slice_in_dim(gathered, position * unknowns, unknowns, 1)

    lifted = precondition(residual)
    mapped = product(lifted)
    lifted_two = precondition(mapped)
    mapped_two = product(lifted_two)
    norm_res, curve_one, square_map, mixed_res, mixed_map, square_two = together(
        (
            dotted(residual, residual),
            dotted(residual, mapped),
            dotted(mapped, mapped),
            dotted(mapped_two, residual),
            dotted(mapped_two, mapped),
            dotted(mapped_two, mapped_two),
        ),
        (("rows_0", "rows_1"), "rows_2"),
    )
    alpha_step = norm_res / curve_one
    cross_mid = (
        curve_one
        - alpha_step * square_map
        - alpha_step * mixed_res
        + alpha_step * alpha_step * mixed_map
    )
    square_mid = square_map - 2.0 * alpha_step * mixed_map + alpha_step * alpha_step * square_two
    middle = residual - alpha_step[:, None] * mapped
    lifted_mid = lifted - alpha_step[:, None] * lifted_two
    mapped_mid = mapped - alpha_step[:, None] * mapped_two
    omega_step = cross_mid / square_mid
    new_iterate = iterate + alpha_step[:, None] * lifted + omega_step[:, None] * lifted_mid
    new_residual = middle - omega_step[:, None] * mapped_mid
    return (new_iterate, new_residual)


def solution(mesh):
    torus = Mesh(
        mesh.devices.reshape(4, 16, 2, mesh.shape["grp"]), ("rows_0", "rows_1", "rows_2", "grp")
    )
    placed = (P(ROWS, "grp"), P(ROWS, None, None), P(ROWS, None), P(None, ROWS), P(None, ROWS))
    return jax.shard_map(
        body, mesh=torus, in_specs=placed, out_specs=(P(None, ROWS), P(None, ROWS)), check_vma=False
    )
```

profile of v0, /device:TPU:1, one launch (start us, length us, event | category | flops | bytes accessed | tf_op | source)
XLA Modules:
  0.0 185.8 jit_solution(15531553699465084661)
XLA Ops:
  0.6 0.0 copy-start
  0.6 0.8 iota_compare_fusion.1
  1.4 0.7 copy.29
  2.2 0.1 reduce.4
  2.3 0.7 bitcast_subtract_fusion
  3.0 0.1 iota_add_fusion
  3.1 1.6 convolution_bitcast_fusion
  4.7 0.0 copy-done
  4.7 0.6 convolution_bitcast_fusion.2
  5.2 0.4 convolution_bitcast_fusion.4
  5.6 4.1 %fusion.18 = f32[6,6144]{1,0:T(8,128)S(1)} fusion(f32[6,192]{1,0:T(8,128)S(1)} %convolution_bitcast_fusion.4, f32[192,6144]{1,0:T(8,128)} %param.5), kind=kOutput, calls=%fused_computation.37 | convolution fusion | flops 84934656 | bytes 4870656 | tf_op jit(solution)/shard_map/dot_general | solution.py:114
  9.8 0.2 reshape_reshape.6
  10.1 10.4 %all_to_all.78 = f32[2,64,288]{2,1,0:T(8,128)S(1)} all-to-all(f32[2,64,288]{2,1,0:T(8,128)S(1)} %bitcast.55), channel_id=1, replica_groups=mesh['rows_0'=4,'rows_1'=16,'rows_2'=2,'grp'=4] {'rows_2'}, dimensions={0} | all-to-all | bytes 294912 | tf_op jit(solution)/shard_map/all_to_all | solution.py:21
  20.4 0.1 all_to_all.51
  20.5 26.5 %all_to_all.79 = f32[64,1,288]{2,1,0:T(1,128)S(1)} all-to-all(f32[64,1,288]{2,1,0:T(1,128)S(1)} %all_to_all.51), channel_id=1, replica_groups=mesh['rows_0'=4,'rows_1'=16,'rows_2'=2,'grp'=4] {'rows_0','rows_1'}, dimensions={0} | all-to-all | bytes 147456 | tf_op jit(solution)/shard_map/all_to_all | solution.py:29
  47.0 0.1 reduce_sum.110
  47.1 0.1 broadcast_in_dim.16
  47.2 20.1 %all_to_all.80 = f32[64,1,288]{2,1,0:T(1,128)S(1)} all-to-all(f32[64,1,288]{2,1,0:T(1,128)S(1)} %broadcast_in_dim.16), channel_id=1, replica_groups=mesh['rows_0'=4,'rows_1'=16,'rows_2'=2,'grp'=4] {'rows_0','rows_1'}, dimensions={0} | all-to-all | bytes 147456 | tf_op jit(solution)/shard_map/all_to_all | solution.py:40
  67.3 6.2 %all_to_all.81 = f32[2,64,288]{2,1,0:T(8,128)S(1)} all-to-all(f32[2,64,288]{2,1,0:T(8,128)S(1)} %broadcast_in_dim.17), channel_id=1, replica_groups=mesh['rows_0'=4,'rows_1'=16,'rows_2'=2,'grp'=4] {'rows_2'}, dimensions={0} | all-to-all | bytes 294912 | tf_op jit(solution)/shard_map/all_to_all | solution.py:40
  73.5 0.2 copy.31
  73.7 0.2 reshape_reshape_reshape.6
  73.9 0.9 broadcast_in_dim.18
  74.9 4.2 %all-to-all-start.4 = ((f32[4,6,6144]{2,1,0:T(8,128)}), f32[4,6,6144]{2,1,0:T(8,128)S(1)}, u32[]{:S(2)}, u32[]{:S(2)}) async-start(f32[4,6,6144]{2,1,0:T(8,128)} %broadcast_in_dim.18), calls=%async_computation.4 | async-start | bytes 1572864 | tf_op jit(solution)/shard_map/all_to_all | solution.py:40
  79.0 11.7 %all-to-all-done.4 = f32[4,6,6144]{2,1,0:T(8,128)S(1)} async-done(((f32[4,6,6144]{2,1,0:T(8,128)}), f32[4,6,6144]{2,1,0:T(8,128)S(1)}, u32[]{:S(2)}, u32[]{:S(2)}) %all-to-all-start.4) | async-done | bytes 589856 | tf_op jit(solution)/shard_map/all_to_all | solution.py:40
  90.8 0.9 fusion.2
  91.7 0.6 convolution_bitcast_fusion.1
  92.3 0.4 convolution_bitcast_fusion.3
  92.7 0.0 copy-start.1
  92.7 0.0 copy-start.2
  92.7 4.1 %fusion.19 = f32[6,6144]{1,0:T(8,128)S(1)} fusion(f32[6,192]{1,0:T(8,128)S(1)} %convolution_bitcast_fusion.3, f32[192,6144]{1,0:T(8,128)} %param.5), kind=kOutput, calls=%fused_computation.38 | convolution fusion | flops 84934656 | bytes 4870656 | tf_op jit(solution)/shard_map/dot_general | solution.py:114
  96.8 0.2 reshape_reshape.7
  97.1 5.0 %all_to_all.82 = f32[2,64,288]{2,1,0:T(8,128)S(1)} all-to-all(f32[2,64,288]{2,1,0:T(8,128)S(1)} %bitcast.57), channel_id=1, replica_groups=mesh['rows_0'=4,'rows_1'=16,'rows_2'=2,'grp'=4] {'rows_2'}, dimensions={0} | all-to-all | bytes 294912 | tf_op jit(solution)/shard_map/all_to_all | solution.py:21
  102.2 0.1 all_to_all.58
  102.2 18.3 %all_to_all.83 = f32[64,1,288]{2,1,0:T(1,128)S(1)} all-to-all(f32[64,1,288]{2,1,0:T(1,128)S(1)} %all_to_all.58), channel_id=1, replica_groups=mesh['rows_0'=4,'rows_1'=16,'rows_2'=2,'grp'=4] {'rows_0','rows_1'}, dimensions={0} | all-to-all | bytes 147456 | tf_op jit(solution)/shard_map/all_to_all | solution.py:29
  120.6 0.1 reduce_sum.114
  120.7 0.1 broadcast_in_dim.19
  120.8 20.1 %all_to_all.84 = f32[64,1,288]{2,1,0:T(1,128)S(1)} all-to-all(f32[64,1,288]{2,1,0:T(1,128)S(1)} %broadcast_in_dim.19), channel_id=1, replica_groups=mesh['rows_0'=4,'rows_1'=16,'rows_2'=2,'grp'=4] {'rows_0','rows_1'}, dimensions={0} | all-to-all | bytes 147456 | tf_op jit(solution)/shard_map/all_to_all | solution.py:40
  140.9 6.2 %all_to_all.85 = f32[2,64,288]{2,1,0:T(8,128)S(1)} all-to-all(f32[2,64,288]{2,1,0:T(8,128)S(1)} %broadcast_in_dim.20), channel_id=1, replica_groups=mesh['rows_0'=4,'rows_1'=16,'rows_2'=2,'grp'=4] {'rows_2'}, dimensions={0} | all-to-all | bytes 294912 | tf_op jit(solution)/shard_map/all_to_all | solution.py:40
  147.1 0.2 copy.33
  147.3 0.2 reshape_reshape_reshape.7
  147.5 0.1 broadcast_in_dim.21
  147.6 14.4 %all_to_all.86 = f32[4,6,6144]{2,1,0:T(8,128)S(1)} all-to-all(f32[4,6,6144]{2,1,0:T(8,128)S(1)} %broadcast_in_dim.21), channel_id=1, replica_groups=mesh['rows_0'=4,'rows_1'=16,'rows_2'=2,'grp'=4] {'grp'}, dimensions={0} | all-to-all | bytes 1179648 | tf_op jit(solution)/shard_map/all_to_all | solution.py:40
  162.0 0.0 copy-done.1
  162.0 0.3 multiply_reduce_fusion
  162.3 0.1 concatenate.3
  162.3 4.6 %all_to_all.87 = f32[2,1,36]{2,1,0:T(1,128)S(1)} all-to-all(f32[2,1,36]{2,1,0:T(1,128)S(1)} %broadcast_in_dim.44), channel_id=1, replica_groups=mesh['rows_0'=4,'rows_1'=16,'rows_2'=2,'grp'=4] {'rows_2'}, dimensions={0} | all-to-all | bytes 576 | tf_op jit(solution)/shard_map/all_to_all | solution.py:40
  167.0 18.0 %all_to_all.88 = f32[64,1,36]{2,1,0:T(1,128)S(1)} all-to-all(f32[64,1,36]{2,1,0:T(1,128)S(1)} %broadcast_in_dim.45), channel_id=1, replica_groups=mesh['rows_0'=4,'rows_1'=16,'rows_2'=2,'grp'=4] {'rows_0','rows_1'}, dimensions={0} | all-to-all | bytes 18432 | tf_op jit(solution)/shard_map/all_to_all | solution.py:40
  184.9 0.1 reduce_sum.119
  185.0 0.1 add_divide_fusion
  185.1 0.0 copy-done.2
  185.1 0.7 multiply_subtract_fusion
  (12 shorter events, 0.2 us)
Async XLA Ops:
  0.6 4.0 %copy-start = (f32[24,24,24]{2,1,0:T(8,128)S(1)}, f32[24,24,24]{2,1,0:T(8,128)}, u32[]{:S(2)}) copy-start(f32[24,24,24]{2,1,0:T(8,128)} %param.6) | copy-start | bytes 165892
  74.9 15.9 %all-to-all-start.4 = ((f32[4,6,6144]{2,1,0:T(8,128)}), f32[4,6,6144]{2,1,0:T(8,128)S(1)}, u32[]{:S(2)}, u32[]{:S(2)}) async-start(f32[4,6,6144]{2,1,0:T(8,128)} %broadcast_in_dim.18), calls=%async_computation.4 | async-start | bytes 1572864 | tf_op jit(solution)/shard_map/all_to_all | solution.py:40
  92.7 69.3 %copy-start.1 = (f32[6,192]{1,0:T(8,128)S(1)}, f32[6,192]{1,0:T(8,128)}, u32[]{:S(2)}) copy-start(f32[6,192]{1,0:T(8,128)} %param.9) | copy-start | bytes 13828
  92.7 92.4 %copy-start.2 = (f32[6,192]{1,0:T(8,128)S(1)}, f32[6,192]{1,0:T(8,128)}, u32[]{:S(2)}) copy-start(f32[6,192]{1,0:T(8,128)} %param.8) | copy-start | bytes 13828
where the time goes:
time: 186 us
  blocking collectives  150 us (81%)
  matrix products  12.8 us (7%)
  waiting for transfers between devices  11.7 us (6%)
  starting transfers between devices  4.18 us (2%)
  local copies, waits for them, and re-layouts  3.44 us (2%)
  other arithmetic  3.04 us (2%)
    all_to_all x7, blocking collectives, from_everyone(): return lax.all_to_all(copies, axis, split_axis=0, concat_axis=0, tiled=True)  89.6 us
    all_to_all x2, blocking collectives, summed_rows(): lax.all_to_all(nearer, far, split_axis=0, concat_axis=0, tiled=True)  44.8 us
    all_to_all x2, blocking collectives, summed_on_arrival(): lax.all_to_all(pieces, axis, split_axis=0, concat_axis=0, tiled=True)  15.4 us
    all_to_all x1, waiting for transfers between devices, from_everyone(): return lax.all_to_all(copies, axis, split_axis=0, concat_axis=0, tiled=True)  11.7 us
    dot_general x2, matrix products, product(): partial_value = jnp.dot(vector, operator, precision=highest)  8.29 us
    all_to_all x1, starting transfers between devices, from_everyone(): return lax.all_to_all(copies, axis, split_axis=0, concat_axis=0, tiled=True)  4.18 us
  transfers between devices with their start and end apart: 1, of which 1 were waited for; matrix products, arithmetic and copies ran while one was open for 0% of the time, Pallas kernels for 0%

commit v1 on v0

v1 whole, which is shorter than its diff:
```python
import jax
import jax.numpy as jnp
from jax import lax
from jax.sharding import Mesh
from jax.sharding import PartitionSpec as P

ROWS = ("x", "z", "c")

highest = lax.Precision.HIGHEST


def exchanged(pieces, axes):
    return lax.all_to_all(pieces, axes, split_axis=0, concat_axis=0, tiled=True)


def selection(lengths, width, depth):
    starts = jnp.cumsum(lengths) - lengths
    offset = jnp.arange(depth, dtype=jnp.int32)
    column = jnp.arange(width, dtype=jnp.int32)
    return (
        (column[None, None, :] == starts[:, None, None] + offset[None, :, None])
        & (offset[None, :, None] < lengths[:, None, None])
    ).astype(jnp.float32)


def block_apply(select, inverse, vector):
    pieces = jnp.einsum("bku,ru->rbk", select, vector, precision=highest)
    solved = jnp.einsum("bkl,rbl->rbk", inverse, pieces, precision=highest)
    return jnp.einsum("bku,rbk->ru", select, solved, precision=highest)


def body(operator, block_inverse, block_len, iterate, residual):
    nx, nz, nc, ny = (lax.axis_size(a) for a in ("x", "z", "c", "y"))
    systems, unknowns = residual.shape
    pair = -(-systems // nx)
    spare = pair * nx - systems
    select = selection(block_len[0], unknowns, block_inverse.shape[1])
    my_x = lax.axis_index("x")

    def pairs(rows):
        return jnp.pad(rows, ((0, spare), (0, 0))).reshape(nx, pair * unknowns)

    def reduced(vector):
        partial_value = jnp.dot(vector, operator, precision=highest)
        padded = jnp.pad(partial_value, ((0, spare), (0, 0)))
        cut = padded.reshape(nx, pair, nz, nc, unknowns).transpose(0, 3, 2, 1, 4)
        cut = cut.reshape(nx * nc, nz, pair * unknowns)
        near = exchanged(cut, ("x", "c")).sum(axis=0)
        far = exchanged(near[:, None, :], "z")
        return far.sum(axis=(0, 1))

    def delivered(pieces):
        arrived = exchanged(pieces.reshape(nx * ny, 1, -1), ("x", "y")).reshape(nx, ny, -1)
        return arrived

    def mine(arrived):
        row = lax.dynamic_index_in_dim(arrived, my_x, 1, keepdims=False)
        return row.reshape(nx * pair, unknowns)[:systems]

    width = pair * unknowns
    lifted = block_apply(select, block_inverse, residual)
    piece = reduced(lifted)
    sent = jnp.concatenate(
        [jnp.broadcast_to(piece, (nx, ny, width)), jnp.broadcast_to(pairs(residual)[:, None], (nx, ny, width))],
        axis=2,
    )
    arrived = delivered(sent)
    mapped = mine(arrived[:, :, :width])
    my_y = lax.axis_index("y")
    other = lax.dynamic_index_in_dim(arrived[:, 0, width:], my_y, 0, keepdims=False)
    lifted_two = block_apply(select, block_inverse, mapped)
    piece_two = reduced(lifted_two)

    r, m, t = (v.reshape(pair, unknowns) for v in (other, piece, piece_two))
    dots = jnp.stack([jnp.sum(a * b, axis=1) for a, b in ((r, r), (r, m), (m, m), (t, r), (t, m), (t, t))])
    tail = jnp.pad(dots.reshape(-1), (0, 128 - dots.size))
    arrived = delivered(jnp.broadcast_to(jnp.concatenate([piece_two, tail]), (nx, ny, width + 128)))
    mapped_two = mine(arrived[:, :, :width])
    near = arrived[:, :, width : width + dots.size].sum(axis=1).reshape(-1)
    totals = exchanged(jnp.broadcast_to(near, (nz * nc, 1, near.size)), ("z", "c")).sum(axis=(0, 1))
    totals = totals.reshape(nx, 6, pair).transpose(1, 0, 2).reshape(6, nx * pair)[:, :systems]
    norm_res, curve_one, square_map, mixed_res, mixed_map, square_two = totals

    alpha_step = norm_res / curve_one
    cross_mid = (
        curve_one
        - alpha_step * square_map
        - alpha_step * mixed_res
        + alpha_step * alpha_step * mixed_map
    )
    square_mid = square_map - 2.0 * alpha_step * mixed_map + alpha_step * alpha_step * square_two
    omega_step = cross_mid / square_mid
    middle = residual - alpha_step[:, None] * mapped
    lifted_mid = lifted - alpha_step[:, None] * lifted_two
    mapped_mid = mapped - alpha_step[:, None] * mapped_two
    new_iterate = iterate + alpha_step[:, None] * lifted + omega_step[:, None] * lifted_mid
    new_residual = middle - omega_step[:, None] * mapped_mid
    return (new_iterate, new_residual)


def solution(mesh):
    torus = Mesh(mesh.devices.reshape(4, 16, 2, mesh.shape["grp"]), ("x", "z", "c", "y"))
    placed = (P(ROWS, "y"), P(ROWS, None, None), P(ROWS, None), P(None, ROWS), P(None, ROWS))
    return jax.shard_map(
        body, mesh=torus, in_specs=placed, out_specs=(P(None, ROWS), P(None, ROWS)), check_vma=False
    )
```

time: 186 us -> 127 us (0.68)
  blocking collectives: 150 us -> 36.4 us
  waiting for transfers between devices: 11.7 us -> 40.6 us
  starting transfers between devices: 4.18 us -> 26.7 us
  local copies, waits for them, and re-layouts: 3.44 us -> 6.02 us
    all_to_all x11 -> x3, blocking collectives: 150 us -> 36.4 us  [exchanged(): return lax.all_to_all(pieces, axes, split_axis=0, concat_axis=0, tiled=True)]
    all_to_all x1 -> x4, waiting for transfers between devices: 11.7 us -> 40.6 us  [exchanged(): return lax.all_to_all(pieces, axes, split_axis=0, concat_axis=0, tiled=True)]
    all_to_all x1 -> x4, starting transfers between devices: 4.18 us -> 26.7 us  [exchanged(): return lax.all_to_all(pieces, axes, split_axis=0, concat_axis=0, tiled=True)]
    reshape x0 -> x16, local copies, waits for them, and re-layouts: none -> 2.55 us  [the longest x4 0.9 us: reduced(): cut = padded.reshape(nx, pair, nz, nc, unknowns).transpose(0, 3, 2, 1, 4)]
  transfers between devices with their start and end apart: 1 -> 4, of which waited for: 1 -> 4; matrix products, arithmetic and copies ran while one was open for 0% -> 0% of each run, Pallas kernels for 0% -> 0%
where the time goes in v1:
time: 127 us; the launch traced here: 126 us
  waiting for transfers between devices  40.6 us (32%)
  blocking collectives  36.4 us (29%)
  starting transfers between devices  26.7 us (21%)
  matrix products  12.8 us (10%)
  local copies, waits for them, and re-layouts  6.02 us (5%)
  other arithmetic  2.91 us (2%)
    all_to_all x4, waiting for transfers between devices, exchanged(): return lax.all_to_all(pieces, axes, split_axis=0, concat_axis=0, tiled=True)  40.6 us
    all_to_all x3, blocking collectives, exchanged(): return lax.all_to_all(pieces, axes, split_axis=0, concat_axis=0, tiled=True)  36.4 us
    all_to_all x4, starting transfers between devices, exchanged(): return lax.all_to_all(pieces, axes, split_axis=0, concat_axis=0, tiled=True)  26.7 us
    dot_general x2, matrix products, reduced(): partial_value = jnp.dot(vector, operator, precision=highest)  8.29 us
  transfers between devices with their start and end apart: 4, of which 4 were waited for; matrix products, arithmetic and copies ran while one was open for 0% of the time, Pallas kernels for 0%

profile of v1, /device:TPU:1, one launch (start us, length us, event | category | flops | bytes accessed | tf_op | source)
XLA Modules:
  0.0 126.2 jit_solution(2395547019199322722)
XLA Ops:
  0.6 0.0 copy-start
  0.6 0.0 copy-start.1
  0.7 0.8 iota_compare_fusion.1
  1.4 0.7 copy.28
  2.2 0.1 reduce
  2.3 0.7 bitcast_subtract_fusion
  3.0 0.1 iota_add_fusion
  3.1 1.6 %convolution_bitcast_fusion = f32[6,24,24]{2,0,1:T(8,128)S(1)} fusion(s32[24,24]{1,0:T(8,128)S(1)} %iota_add_fusion, pred[24,24]{1,0:T(8,128)(4,1)S(1)} %iota_compare_fusion.1, f32[6,192]{1,0:T(8,128)} %param.9), kind=kOutput, calls=%fused_computation | convolution fusion | flops 8183808 | bytes 21312 | tf_op jit(solution)/shard_map/bku,ru->rbk/dot_general | solution.py:27
  4.7 0.0 copy-done
  4.7 0.6 convolution_bitcast_fusion.2
  5.2 0.4 convolution_bitcast_fusion.4
  5.6 4.1 %fusion.15 = f32[6,6144]{1,0:T(8,128)S(1)} fusion(f32[6,192]{1,0:T(8,128)S(1)} %convolution_bitcast_fusion.4, f32[192,6144]{1,0:T(8,128)} %param.5), kind=kOutput, calls=%fused_computation.44 | convolution fusion | flops 84934656 | bytes 4870656 | tf_op jit(solution)/shard_map/dot_general | solution.py:44
  9.8 0.2 reshape.205
  10.1 0.2 copy.38
  10.3 0.2 reshape.206
  10.5 15.1 %all_to_all.35 = f32[8,16,384]{2,1,0:T(8,128)S(1)} all-to-all(f32[8,16,384]{2,1,0:T(8,128)S(1)} %reshape.206), channel_id=1, replica_groups=mesh['x'=4,'z'=16,'c'=2,'y'=4] {'x','c'}, dimensions={0} | all-to-all | bytes 393216 | tf_op jit(solution)/shard_map/all_to_all | solution.py:13
  25.6 0.6 broadcast_in_dim.12
  26.2 11.3 %all-to-all-start.1 = ((f32[16,1,384]{2,1,0:T(1,128)}), f32[16,1,384]{2,1,0:T(1,128)S(1)}, u32[]{:S(2)}, u32[]{:S(2)}) async-start(f32[16,1,384]{2,1,0:T(1,128)} %broadcast_in_dim.12), calls=%async_computation.1 | async-start | bytes 49152 | tf_op jit(solution)/shard_map/all_to_all | solution.py:13
  37.5 0.0 copy-done.1
  37.5 0.1 broadcast_in_dim.14
  37.6 11.3 %all-to-all-done.1 = f32[16,1,384]{2,1,0:T(1,128)S(1)} async-done(((f32[16,1,384]{2,1,0:T(1,128)}), f32[16,1,384]{2,1,0:T(1,128)S(1)}, u32[]{:S(2)}, u32[]{:S(2)}) %all-to-all-start.1) | async-done | bytes 24608 | tf_op jit(solution)/shard_map/all_to_all | solution.py:13
  49.0 0.7 reshape.207
  49.7 4.9 %all-to-all-start.2 = ((f32[16,1,768]{2,1,0:T(1,128)}), f32[16,1,768]{2,1,0:T(1,128)S(1)}, u32[]{:S(2)}, u32[]{:S(2)}) async-start(f32[16,1,768]{2,1,0:T(1,128)} %reshape.207), calls=%async_computation.2 | async-start | bytes 98304 | tf_op jit(solution)/shard_map/all_to_all | solution.py:13
  54.6 6.5 %all-to-all-done.2 = f32[16,1,768]{2,1,0:T(1,128)S(1)} async-done(((f32[16,1,768]{2,1,0:T(1,128)}), f32[16,1,768]{2,1,0:T(1,128)S(1)}, u32[]{:S(2)}, u32[]{:S(2)}) %all-to-all-start.2) | async-done | bytes 49184 | tf_op jit(solution)/shard_map/all_to_all | solution.py:13
  61.1 0.1 reduce.1
  61.2 0.0 copy-start.2
  61.3 0.1 reshape.222
  61.3 0.9 fusion.2
  62.3 0.6 convolution_bitcast_fusion.1
  62.8 0.4 convolution_bitcast_fusion.3
  63.2 4.1 %fusion.16 = f32[6,6144]{1,0:T(8,128)S(1)} fusion(f32[6,192]{1,0:T(8,128)S(1)} %convolution_bitcast_fusion.3, f32[192,6144]{1,0:T(8,128)} %param.5), kind=kOutput, calls=%fused_computation.45 | convolution fusion | flops 84934656 | bytes 4870656 | tf_op jit(solution)/shard_map/dot_general | solution.py:44
  67.4 0.2 reshape.209
  67.7 0.2 copy.37
  67.9 0.2 reshape.210
  68.1 12.1 %all_to_all.36 = f32[8,16,384]{2,1,0:T(8,128)S(1)} all-to-all(f32[8,16,384]{2,1,0:T(8,128)S(1)} %reshape.210), channel_id=1, replica_groups=mesh['x'=4,'z'=16,'c'=2,'y'=4] {'x','c'}, dimensions={0} | all-to-all | bytes 393216 | tf_op jit(solution)/shard_map/all_to_all | solution.py:13
  80.1 0.6 broadcast_in_dim.16
  80.8 3.5 %all-to-all-start.4 = ((f32[16,1,384]{2,1,0:T(1,128)}), f32[16,1,384]{2,1,0:T(1,128)S(1)}, u32[]{:S(2)}, u32[]{:S(2)}) async-start(f32[16,1,384]{2,1,0:T(1,128)} %broadcast_in_dim.16), calls=%async_computation.4 | async-start | bytes 49152 | tf_op jit(solution)/shard_map/all_to_all | solution.py:13
  84.3 0.1 reshape.212
  84.4 0.1 reshape.211
  84.5 11.0 %all-to-all-done.4 = f32[16,1,384]{2,1,0:T(1,128)S(1)} async-done(((f32[16,1,384]{2,1,0:T(1,128)}), f32[16,1,384]{2,1,0:T(1,128)S(1)}, u32[]{:S(2)}, u32[]{:S(2)}) %all-to-all-start.4) | async-done | bytes 24608 | tf_op jit(solution)/shard_map/all_to_all | solution.py:13
  95.5 0.1 reshape.213
  95.6 0.2 multiply_reduce_fusion
  95.8 0.1 reshape.214
  95.9 9.3 %all_to_all.37 = f32[16,1,512]{2,1,0:T(1,128)S(1)} all-to-all(f32[16,1,512]{2,1,0:T(1,128)S(1)} %reshape.215), channel_id=1, replica_groups=mesh['x'=4,'z'=16,'c'=2,'y'=4] {'x','y'}, dimensions={0} | all-to-all | bytes 65536 | tf_op jit(solution)/shard_map/all_to_all | solution.py:13
  105.3 0.1 reduce.4
  105.4 0.1 reshape.217
  105.5 0.6 broadcast_in_dim.17
  106.1 7.0 %all-to-all-start.6 = ((f32[32,1,48]{2,1,0:T(1,128)}), f32[32,1,48]{2,1,0:T(1,128)S(1)}, u32[]{:S(2)}, u32[]{:S(2)}) async-start(f32[32,1,48]{2,1,0:T(1,128)} %broadcast_in_dim.17), calls=%async_computation.6 | async-start | bytes 32768 | tf_op jit(solution)/shard_map/all_to_all | solution.py:13
  113.1 0.1 slice.33
  113.2 0.1 slice.38
  113.3 11.7 %all-to-all-done.6 = f32[32,1,48]{2,1,0:T(1,128)S(1)} async-done(((f32[32,1,48]{2,1,0:T(1,128)}), f32[32,1,48]{2,1,0:T(1,128)S(1)}, u32[]{:S(2)}, u32[]{:S(2)}) %all-to-all-start.6) | async-done | bytes 6176 | tf_op jit(solution)/shard_map/all_to_all | solution.py:13
  125.0 0.1 reshape.218
  125.1 0.1 copy.32
  125.3 0.3 slice_reduce_fusion.3
  125.5 0.0 copy-done.2
  125.5 0.7 multiply_subtract_fusion
  (25 shorter events, 0.5 us)
Async XLA Ops:
  0.6 4.0 %copy-start = (f32[24,24,24]{2,1,0:T(8,128)S(1)}, f32[24,24,24]{2,1,0:T(8,128)}, u32[]{:S(2)}) copy-start(f32[24,24,24]{2,1,0:T(8,128)} %param.6) | copy-start | bytes 165892
  0.6 36.8 %copy-start.1 = (f32[6,192]{1,0:T(8,128)S(1)}, f32[6,192]{1,0:T(8,128)}, u32[]{:S(2)}) copy-start(f32[6,192]{1,0:T(8,128)} %param.9) | copy-start | bytes 13828
  26.2 22.7 %all-to-all-start.1 = ((f32[16,1,384]{2,1,0:T(1,128)}), f32[16,1,384]{2,1,0:T(1,128)S(1)}, u32[]{:S(2)}, u32[]{:S(2)}) async-start(f32[16,1,384]{2,1,0:T(1,128)} %broadcast_in_dim.12), calls=%async_computation.1 | async-start | bytes 49152 | tf_op jit(solution)/shard_map/all_to_all | solution.py:13
  49.7 11.4 %all-to-all-start.2 = ((f32[16,1,768]{2,1,0:T(1,128)}), f32[16,1,768]{2,1,0:T(1,128)S(1)}, u32[]{:S(2)}, u32[]{:S(2)}) async-start(f32[16,1,768]{2,1,0:T(1,128)} %reshape.207), calls=%async_computation.2 | async-start | bytes 98304 | tf_op jit(solution)/shard_map/all_to_all | solution.py:13
  61.2 64.3 %copy-start.2 = (f32[6,192]{1,0:T(8,128)S(1)}, f32[6,192]{1,0:T(8,128)}, u32[]{:S(2)}) copy-start(f32[6,192]{1,0:T(8,128)} %param.8) | copy-start | bytes 13828
  80.8 14.7 %all-to-all-start.4 = ((f32[16,1,384]{2,1,0:T(1,128)}), f32[16,1,384]{2,1,0:T(1,128)S(1)}, u32[]{:S(2)}, u32[]{:S(2)}) async-start(f32[16,1,384]{2,1,0:T(1,128)} %broadcast_in_dim.16), calls=%async_computation.4 | async-start | bytes 49152 | tf_op jit(solution)/shard_map/all_to_all | solution.py:13
  106.1 19.0 %all-to-all-start.6 = ((f32[32,1,48]{2,1,0:T(1,128)}), f32[32,1,48]{2,1,0:T(1,128)S(1)}, u32[]{:S(2)}, u32[]{:S(2)}) async-start(f32[32,1,48]{2,1,0:T(1,128)} %broadcast_in_dim.17), calls=%async_computation.6 | async-start | bytes 32768 | tf_op jit(solution)/shard_map/all_to_all | solution.py:13

commit v2 on v1

v2 whole, which is shorter than its diff:
```python
import functools

import jax
import jax.numpy as jnp
from jax import lax
from jax.experimental import pallas as pl
from jax.experimental.pallas import tpu as pltpu
from jax.sharding import Mesh
from jax.sharding import PartitionSpec as P

ROWS = ("x", "z", "c")
NX, NZ, NC, NY = 4, 16, 2, 4
SYS, UNK, LANE = 6, 192, 128
REST = UNK - LANE
PAIR = 2
WIDE = PAIR * UNK
TILES = WIDE // LANE
BLOCKS = 24
COPIES = 4
DOTS = 6

highest = lax.Precision.HIGHEST
f32 = jnp.float32
VM = pl.BlockSpec(memory_space=pltpu.VMEM)


def iota(shape, dim):
    return lax.broadcasted_iota(jnp.int32, shape, dim)


def nt(a, b):
    return lax.dot_general(a, b, (((1,), (1,)), ((), ())), precision=highest, preferred_element_type=f32)


def preconditioner(len_ref, inverse):
    slots = BLOCKS * BLOCKS
    slot = iota((1, slots), 1)
    block = slot // BLOCKS
    within = slot - block * BLOCKS
    column = iota((1, UNK), 1)
    target = jnp.full((1, slots), -1, jnp.int32)
    first = jnp.zeros((1, UNK), jnp.int32)
    last = jnp.zeros((1, UNK), jnp.int32)
    start = jnp.int32(0)
    for b in range(BLOCKS):
        size = len_ref[0, b]
        end = start + size
        target = jnp.where((block == b) & (within < size), start + within, target)
        inside = (column >= start) & (column < end)
        first = jnp.where(inside, start, first)
        last = jnp.where(inside, end, last)
        start = end
    pick = (iota((UNK, slots), 0) == target).astype(f32)
    rows = jnp.dot(pick, inverse, precision=highest, preferred_element_type=f32)
    spread = (iota((BLOCKS, UNK), 0) == column - first).astype(f32)
    full = jnp.dot(rows, spread, precision=highest, preferred_element_type=f32)
    row = iota((UNK, UNK), 0)
    return jnp.where((row >= first) & (row < last), full, 0.0)


def encoded(vector, core):
    main = jnp.where(core == 0, vector[:, :LANE], vector[:, REST:])
    rest = jnp.where(core == 0, vector[:, LANE:], vector[:, :REST])
    rows = []
    for p in range(SYS // PAIR):
        a, b = PAIR * p, PAIR * p + 1
        rows.append(jnp.concatenate([main[a : a + 1], main[b : b + 1], rest[a : a + 1], rest[b : b + 1]], axis=1))
    return rows


def decoded(rows, core):
    main = jnp.concatenate([r[:, k * LANE : (k + 1) * LANE] for r in rows for k in range(PAIR)], axis=0)
    rest = jnp.concatenate(
        [r[:, PAIR * LANE + k * REST : PAIR * LANE + (k + 1) * REST] for r in rows for k in range(PAIR)], axis=0
    )
    return jnp.where(
        core == 0, jnp.concatenate([main, rest], axis=1), jnp.concatenate([rest, main], axis=1)
    )


def copies_of(operator_ref, held, sems):
    width = operator_ref.shape[1] // COPIES
    return [
        pltpu.make_async_copy(
            operator_ref.at[:, k * width : (k + 1) * width], held.at[:, k * width : (k + 1) * width], sems.at[k]
        )
        for k in range(COPIES)
    ]


def product(matrix, vector, copies, held, spread, cut_ref):
    turned = nt(matrix, vector)
    for s in range(SYS):
        spread[s] = jnp.broadcast_to(turned[:, s : s + 1], (UNK, LANE))
    for k in range(SYS // PAIR, NX):
        for c in range(NC):
            cut_ref[k * NC + c] = jnp.zeros((NZ, 1, WIDE), f32)
    low = iota((1, LANE), 1) < REST

    def one(z, carry):
        base = pl.multiple_of(z * (NC * UNK), LANE)
        totals = [[None] * TILES for _ in range(SYS)]
        for j in range(UNK // 8):
            tiles = [held[8 * j : 8 * j + 8, pl.ds(base + k * LANE, LANE)] for k in range(TILES)]
            for s in range(SYS):
                v = spread[s, 8 * j : 8 * j + 8, :]
                for k in range(TILES):
                    term = tiles[k] * v
                    totals[s][k] = term if j == 0 else totals[s][k] + term
        sums = [[jnp.sum(totals[s][k], axis=0, keepdims=True) for k in range(TILES)] for s in range(SYS)]
        for p in range(SYS // PAIR):
            a, b = sums[PAIR * p], sums[PAIR * p + 1]
            lo = jnp.where(low, a[1], pltpu.roll(b[1], REST, 1))
            hi = jnp.where(low, pltpu.roll(a[1], REST, 1), b[1])
            for c, row in ((0, (a[0], b[0], lo)), (1, (a[2], b[2], hi))):
                for k in range(TILES):
                    cut_ref[NC * p + c, z, :, k * LANE : (k + 1) * LANE] = row[k]
        return carry

    per = NZ // COPIES
    for k in range(COPIES):
        copies[k].wait()
        lax.fori_loop(k * per, (k + 1) * per, one, 0)


def first_kernel(
    len_hbm, inverse_hbm, residual_hbm, iterate_hbm, operator_hbm,
    cut_ref, matrix_ref, lifted_ref, ride_ref, residual_ref, iterate_ref,
    held, spread, sems, lengths, inverse, small_sems,
):
    small = [
        pltpu.make_async_copy(source, target, small_sems.at[k])
        for k, (source, target) in enumerate(
            ((len_hbm, lengths), (inverse_hbm, inverse), (residual_hbm, residual_ref), (iterate_hbm, iterate_ref))
        )
    ]
    for copy in small:
        copy.start()
    copies = copies_of(operator_hbm, held, sems)
    for copy in copies:
        copy.start()
    for copy in small:
        copy.wait()
    core = lax.axis_index("c")
    residual = residual_ref[...]
    matrix = preconditioner(lengths, inverse[...])
    product(matrix, residual, copies, held, spread, cut_ref)
    matrix_ref[...] = matrix
    lifted_ref[...] = nt(residual, matrix)
    rows = encoded(residual, core)
    for x in range(NX):
        row = rows[x] if x < len(rows) else jnp.zeros((1, WIDE), f32)
        for y in range(NY):
            ride_ref[x * NY + y] = row


def second_kernel(
    arrived_ref, matrix_ref, operator_hbm, cut_ref, mapped_ref, lifted_ref, piece_ref, other_ref, held, spread, sems
):
    copies = copies_of(operator_hbm, held, sems)
    for copy in copies:
        copy.start()
    core, x, y = lax.axis_index("c"), lax.axis_index("x"), lax.axis_index("y")
    mapped = decoded([arrived_ref[p * NY + x][:, :WIDE] for p in range(SYS // PAIR)], core)
    matrix = matrix_ref[...]
    product(matrix, mapped, copies, held, spread, cut_ref)
    mapped_ref[...] = mapped
    lifted_ref[...] = nt(mapped, matrix)
    piece_ref[...] = arrived_ref[x * NY + y][:, :WIDE]
    other_ref[...] = arrived_ref[y * NY][:, WIDE:]


def dots_kernel(far_ref, piece_ref, other_ref, sent_ref):
    t = jnp.sum(far_ref[...], axis=0)
    m, r = piece_ref[...], other_ref[...]
    terms = jnp.concatenate([r * r, r * m, m * m, t * r, t * m, t * t], axis=0)
    shared = terms[:, PAIR * LANE :]
    low = iota(shared.shape, 1) < REST
    sides = jnp.concatenate(
        [terms[:, :LANE] + jnp.where(low, shared, 0.0), terms[:, LANE : 2 * LANE] + jnp.where(low, 0.0, shared)], axis=0
    )
    column = jnp.sum(sides, axis=1, keepdims=True)
    shape = (PAIR * DOTS, LANE)
    line = jnp.sum(jnp.where(iota(shape, 0) == iota(shape, 1), column, 0.0), axis=0, keepdims=True)
    row = jnp.concatenate([t, line], axis=1)
    for k in range(NX * NY):
        sent_ref[k] = row


def near_kernel(arrived_ref, sent_ref):
    total = None
    for x in range(NX):
        line = None
        for y in range(NY):
            part = arrived_ref[x * NY + y][:, WIDE:]
            line = part if line is None else line + part
        if x:
            line = pltpu.roll(line, x * PAIR * DOTS, 1)
        total = line if total is None else total + line
    for k in range(NZ * NC):
        sent_ref[k] = total


def last_kernel(far_ref, arrived_ref, iterate_ref, residual_ref, mapped_ref, lifted_ref, lifted_two_ref, new_iterate_ref, new_residual_ref):
    core, x = lax.axis_index("c"), lax.axis_index("x")
    totals = jnp.sum(far_ref[...], axis=0)
    lane = iota((SYS, LANE), 1)
    system = iota((SYS, LANE), 0)
    home = (system // PAIR) * (PAIR * DOTS) + (system % PAIR) * DOTS
    norm_res, curve_one, square_map, mixed_res, mixed_map, square_two = (
        jnp.sum(jnp.where(lane == home + d, totals, 0.0), axis=1, keepdims=True) for d in range(DOTS)
    )
    alpha = norm_res / curve_one
    cross_mid = curve_one - alpha * square_map - alpha * mixed_res + alpha * alpha * mixed_map
    square_mid = square_map - 2.0 * alpha * mixed_map + alpha * alpha * square_two
    omega = cross_mid / square_mid
    mapped, lifted = mapped_ref[...], lifted_ref[...]
    mapped_two = decoded([arrived_ref[p * NY + x][:, :WIDE] for p in range(SYS // PAIR)], core)
    middle = residual_ref[...] - alpha * mapped
    lifted_mid = lifted - alpha * lifted_two_ref[...]
    new_iterate_ref[...] = iterate_ref[...] + alpha * lifted + omega * lifted_mid
    new_residual_ref[...] = middle - omega * (mapped - alpha * mapped_two)


def exchanged(pieces, axes):
    return lax.all_to_all(pieces, axes, split_axis=0, concat_axis=0, tiled=True)


def body(operator, block_inverse, block_len, iterate, residual):
    def shape(*lengths):
        return jax.ShapeDtypeStruct(lengths, f32)

    hbm = pl.BlockSpec(memory_space=pltpu.HBM)
    cut_shape = shape(NX * NC, NZ, 1, WIDE)
    small = shape(SYS, UNK)
    row = shape(1, WIDE)
    scratch = [
        pltpu.VMEM(operator.shape, f32),
        pltpu.VMEM((SYS, UNK, LANE), f32),
        pltpu.SemaphoreType.DMA((COPIES,)),
    ]
    params = pltpu.CompilerParams(vmem_limit_bytes=16 << 20)
    light = pltpu.CompilerParams(vmem_limit_bytes=4 << 20)
    inputs = (block_len, block_inverse.reshape(BLOCKS * BLOCKS, BLOCKS), residual, iterate, operator)
    inputs = [pltpu.with_memory_space_constraint(a, pltpu.HBM) for a in inputs]

    cut, matrix, lifted, ride, residual, iterate = pl.pallas_call(
        first_kernel,
        out_shape=(cut_shape, shape(UNK, UNK), small, shape(NX * NY, 1, WIDE), small, small),
        in_specs=[hbm] * 5,
        out_specs=[VM] * 6,
        scratch_shapes=scratch
        + [
            pltpu.SMEM((1, BLOCKS), jnp.int32),
            pltpu.VMEM((BLOCKS * BLOCKS, BLOCKS), f32),
            pltpu.SemaphoreType.DMA((4,)),
        ],
        compiler_params=params,
        name="first_product",
    )(*inputs)

    def reduced(cut):
        near = exchanged(cut, ("x", "c")).sum(axis=0)
        return exchanged(near, "z")

    piece = reduced(cut).sum(axis=0)
    sent = jnp.concatenate([jnp.broadcast_to(piece[None], ride.shape), ride], axis=2)
    arrived = exchanged(sent, ("x", "y"))

    cut, mapped, lifted_two, piece, other = pl.pallas_call(
        second_kernel,
        out_shape=(cut_shape, small, small, row, row),
        in_specs=[VM, VM, hbm],
        out_specs=[VM] * 5,
        scratch_shapes=scratch,
        compiler_params=params,
        name="second_product",
    )(arrived, matrix, inputs[4])

    sent = pl.pallas_call(
        dots_kernel,
        out_shape=shape(NX * NY, 1, WIDE + LANE),
        in_specs=[VM] * 3,
        out_specs=VM,
        compiler_params=light,
        name="dots",
    )(reduced(cut), piece, other)
    arrived = exchanged(sent, ("x", "y"))
    sent = pl.pallas_call(
        near_kernel,
        out_shape=shape(NZ * NC, 1, LANE),
        in_specs=[VM],
        out_specs=VM,
        compiler_params=light,
        name="near_dots",
    )(arrived)
    far = exchanged(sent, ("z", "c"))
    return tuple(
        pl.pallas_call(
            last_kernel,
            out_shape=(small, small),
            in_specs=[VM] * 7,
            out_specs=[VM] * 2,
            compiler_params=light,
            name="update",
        )(far, arrived, iterate, residual, mapped, lifted, lifted_two)
    )


def solution(mesh):
    torus = Mesh(mesh.devices.reshape(NX, NZ, NC, NY), ("x", "z", "c", "y"))
    placed = (P(ROWS, "y"), P(ROWS, None, None), P(ROWS, None), P(None, ROWS), P(None, ROWS))
    return jax.shard_map(
        body, mesh=torus, in_specs=placed, out_specs=(P(None, ROWS), P(None, ROWS)), check_vma=False
    )
```

time: 127 us -> 115 us (0.906)
  blocking collectives: 36.4 us -> 102 us
  waiting for transfers between devices: 40.6 us -> 0 us
  starting transfers between devices: 26.7 us -> 0 us
  matrix products: 12.8 us -> 0 us
  Pallas kernels: 0 us -> 11.9 us
  local copies, waits for them, and re-layouts: 6.02 us -> 0.04 us
  other arithmetic: 2.91 us -> 0.37 us
    all_to_all x3 -> x7, blocking collectives: 36.4 us -> 102 us  [exchanged(): return lax.all_to_all(pieces, axes, split_axis=0, concat_axis=0, tiled=True)]
    all_to_all x4 -> x0, waiting for transfers between devices: 40.6 us -> none  [exchanged(): return lax.all_to_all(pieces, axes, split_axis=0, concat_axis=0, tiled=True)]
    all_to_all x4 -> x0, starting transfers between devices: 26.7 us -> none  [exchanged(): return lax.all_to_all(pieces, axes, split_axis=0, concat_axis=0, tiled=True)]
    dot_general x8 -> x0, matrix products: 12.8 us -> none  [the longest x2 8.29 us: reduced(): partial_value = jnp.dot(vector, operator, precision=highest)]
    pallas_call x0 -> x5, Pallas kernels: none -> 11.9 us  [the longest x1 6.63 us: body(): pl.pallas_call(first_kernel, out_shape=(cut_shape, shape(UNK, UNK), small...]
    reshape x16 -> x0, local copies, waits for them, and re-layouts: 2.55 us -> none  [the longest x4 0.9 us: reduced(): cut = padded.reshape(nx, pair, nz, nc, unknowns).transpose(0, 3, 2, 1, 4)]
    broadcast_in_dim x5 -> x0, local copies, waits for them, and re-layouts: 1.92 us -> none  [the longest x2 1.23 us: reduced(): far = exchanged(near[:, None, :], 'z')]
    sub x2 -> x0, other arithmetic: 1.34 us -> none  [the longest x1 0.68 us: body(): new_residual = middle - omega_step[:, None] * mapped_mid]
  transfers between devices with their start and end apart: 4 -> 0, of which waited for: 4 -> 0; matrix products, arithmetic and copies ran while one was open for 0% -> 0% of each run, Pallas kernels for 0% -> 0%
where the time goes in v2:
time: 115 us
  blocking collectives  102 us (89%)
  Pallas kernels  11.9 us (10%)
    all_to_all x7, blocking collectives, exchanged(): return lax.all_to_all(pieces, axes, split_axis=0, concat_axis=0, tiled=True)  102 us
    pallas_call x1, Pallas kernels, body(): pl.pallas_call(first_kernel, out_shape=(cut_shape, shape(UNK, UNK), small...  6.63 us
    pallas_call x1, Pallas kernels, body(): pl.pallas_call(second_kernel, out_shape=(cut_shape, small, small, row, ro...  4.32 us

profile of v2, /device:TPU:1, one launch (start us, length us, event | category | flops | bytes accessed | tf_op | source)
XLA Modules:
  0.0 115.0 jit_solution(14554393656566629880)
XLA Ops:
  0.6 6.6 %first_product.1 = (f32[8,16,1,384]{3,2,1,0:T(1,128)S(1)}, f32[192,192]{1,0:T(8,128)S(1)}, f32[6,192]{1,0:T(8,128)S(1)}, f32[16,1,384]{2,1,0:T(1,128)S(1)}, f32[6,192]{1,0:T(8,128)S(1)}, /*index=5*/f32[6,192]{1,0:T(8,128)S(1)}) custom-call(s32[1,24]{1,0:T(1,128)} %len_hbm.1, f32[576,24]{1,0:T(8,128)} %bitcast.1, f32[6,192]{1,0:T(8,128)} %residual_hbm.1, ...), custom_call_target="tpu_custom_call" | custom-call | tf_op jit(solution)/shard_map/first_product/pallas_call | solution.py:247
  7.3 15.1 %all_to_all.35 = f32[8,16,1,384]{3,2,1,0:T(1,128)S(1)} all-to-all(f32[8,16,1,384]{3,2,1,0:T(1,128)S(1)} %get-tuple-element.13), channel_id=1, replica_groups=mesh['x'=4,'z'=16,'c'=2,'y'=4] {'x','c'}, dimensions={0} | all-to-all | bytes 393216 | tf_op jit(solution)/shard_map/all_to_all | solution.py:226
  22.4 0.1 reduce_sum.31
  22.5 22.5 %all_to_all.36 = f32[16,1,384]{2,1,0:T(1,128)S(1)} all-to-all(f32[16,1,384]{2,1,0:T(1,128)S(1)} %reduce_sum.32), channel_id=1, replica_groups=mesh['x'=4,'z'=16,'c'=2,'y'=4] {'z'}, dimensions={0} | all-to-all | bytes 49152 | tf_op jit(solution)/shard_map/all_to_all | solution.py:226
  45.1 11.2 %all_to_all.37.arrived_ref = f32[16,1,768]{2,1,0:T(1,128)S(1)} all-to-all(f32[16,1,768]{2,1,0:T(1,128)S(1)} %pad_maximum_fusion), channel_id=1, replica_groups=mesh['x'=4,'z'=16,'c'=2,'y'=4] {'x','y'}, dimensions={0} | all-to-all | bytes 98304 | tf_op jit(solution)/shard_map/all_to_all | solution.py:226
  56.3 4.3 %second_product.1 = (f32[8,16,1,384]{3,2,1,0:T(1,128)S(1)}, f32[6,192]{1,0:T(8,128)S(1)}, f32[6,192]{1,0:T(8,128)S(1)}, f32[1,384]{1,0:T(1,128)S(1)}, f32[1,384]{1,0:T(1,128)S(1)}) custom-call(f32[16,1,768]{2,1,0:T(1,128)S(1)} %all_to_all.37.arrived_ref, f32[192,192]{1,0:T(8,128)S(1)} %get-tuple-element.15.matrix_ref, f32[192,6144]{1,0:T(8,128)} %operator_hbm.3), custom_call_target="tpu_custom_call" | custom-call | tf_op jit(solution)/shard_map/second_product/pallas_call | solution.py:270
  60.6 12.1 %all_to_all.38 = f32[8,16,1,384]{3,2,1,0:T(1,128)S(1)} all-to-all(f32[8,16,1,384]{3,2,1,0:T(1,128)S(1)} %get-tuple-element.16), channel_id=1, replica_groups=mesh['x'=4,'z'=16,'c'=2,'y'=4] {'x','c'}, dimensions={0} | all-to-all | bytes 393216 | tf_op jit(solution)/shard_map/all_to_all | solution.py:226
  72.7 0.1 reduce_sum.34
  72.9 13.8 %all_to_all.39.far_ref = f32[16,1,384]{2,1,0:T(1,128)S(1)} all-to-all(f32[16,1,384]{2,1,0:T(1,128)S(1)} %reduce_sum.35), channel_id=1, replica_groups=mesh['x'=4,'z'=16,'c'=2,'y'=4] {'z'}, dimensions={0} | all-to-all | bytes 49152 | tf_op jit(solution)/shard_map/all_to_all | solution.py:226
  86.7 0.1 dots.1
  86.8 9.3 %all_to_all.40.arrived_ref = f32[16,1,512]{2,1,0:T(1,128)S(1)} all-to-all(f32[16,1,512]{2,1,0:T(1,128)S(1)} %dots.1), channel_id=1, replica_groups=mesh['x'=4,'z'=16,'c'=2,'y'=4] {'x','y'}, dimensions={0} | all-to-all | bytes 65536 | tf_op jit(solution)/shard_map/all_to_all | solution.py:226
  96.1 0.1 near_dots.1
  96.2 18.1 %all_to_all.41.far_ref = f32[32,1,128]{2,1,0:T(1,128)S(1)} all-to-all(f32[32,1,128]{2,1,0:T(1,128)S(1)} %near_dots.1), channel_id=1, replica_groups=mesh['x'=4,'z'=16,'c'=2,'y'=4] {'z','c'}, dimensions={0} | all-to-all | bytes 32768 | tf_op jit(solution)/shard_map/all_to_all | solution.py:226
  114.3 0.8 update.1
  (5 shorter events, 0.1 us)

commit v3 on v2

--- a/solution.py
+++ b/solution.py
@@ -8,8 +8,10 @@
 from jax.sharding import Mesh
 from jax.sharding import PartitionSpec as P
 
-ROWS = ("x", "z", "c")
-NX, NZ, NC, NY = 4, 16, 2, 4
+Z = ("zh", "zl")
+ROWS = ("x", *Z, "c")
+NX, NH, NL, NC, NY = 4, 8, 2, 2, 4
+NZ = NH * NL
 SYS, UNK, LANE = 6, 192, 128
 REST = UNK - LANE
 PAIR = 2
@@ -89,12 +91,13 @@
 
 
 def product(matrix, vector, copies, held, spread, cut_ref):
+    steps = cut_ref.shape[1]
+    inner = NZ // steps
     turned = nt(matrix, vector)
     for s in range(SYS):
         spread[s] = jnp.broadcast_to(turned[:, s : s + 1], (UNK, LANE))
-    for k in range(SYS // PAIR, NX):
-        for c in range(NC):
-            cut_ref[k * NC + c] = jnp.zeros((NZ, 1, WIDE), f32)
+    for k in range(SYS // PAIR * inner * NC, NX * inner * NC):
+        cut_ref[k] = jnp.zeros((steps, 1, WIDE), f32)
     low = iota((1, LANE), 1) < REST
 
     def one(z, carry):
@@ -114,7 +117,8 @@
             hi = jnp.where(low, pltpu.roll(a[1], REST, 1), b[1])
             for c, row in ((0, (a[0], b[0], lo)), (1, (a[2], b[2], hi))):
                 for k in range(TILES):
-                    cut_ref[NC * p + c, z, :, k * LANE : (k + 1) * LANE] = row[k]
+                    home = (p * inner + lax.rem(z, inner)) * NC + c
+                    cut_ref[home, lax.div(z, inner), :, k * LANE : (k + 1) * LANE] = row[k]
         return carry
 
     per = NZ // COPIES
@@ -170,10 +174,27 @@
     other_ref[...] = arrived_ref[y * NY][:, WIDE:]
 
 
-def dots_kernel(far_ref, piece_ref, other_ref, sent_ref):
-    t = jnp.sum(far_ref[...], axis=0)
-    m, r = piece_ref[...], other_ref[...]
-    terms = jnp.concatenate([r * r, r * m, m * m, t * r, t * m, t * t], axis=0)
+def share_kernel(arrived_ref, piece_ref, other_ref, sent_ref):
+    near = jnp.sum(arrived_ref[...], axis=0)
+    for k in range(NH):
+        sent_ref[k, :NH] = near
+        sent_ref[k, NH] = piece_ref[...]
+        sent_ref[k, NH + 1] = other_ref[...]
+
+
+def dots_kernel(far_ref, sent_ref):
+    mine = far_ref[0, lax.axis_index("zh")]
+    for k in range(1, NH):
+        mine = mine + far_ref[k, lax.axis_index("zh")]
+    terms = [None] * DOTS
+    for h in range(NH):
+        t = far_ref[0, h]
+        for k in range(1, NH):
+            t = t + far_ref[k, h]
+        m, r = far_ref[h, NH], far_ref[h, NH + 1]
+        for d, term in enumerate((r * r, r * m, m * m, t * r, t * m, t * t)):
+            terms[d] = term if h == 0 else terms[d] + term
+    terms = jnp.concatenate(terms, axis=0)
     shared = terms[:, PAIR * LANE :]
     low = iota(shared.shape, 1) < REST
     sides = jnp.concatenate(
@@ -182,28 +203,20 @@
     column = jnp.sum(sides, axis=1, keepdims=True)
     shape = (PAIR * DOTS, LANE)
     line = jnp.sum(jnp.where(iota(shape, 0) == iota(shape, 1), column, 0.0), axis=0, keepdims=True)
-    row = jnp.concatenate([t, line], axis=1)
-    for k in range(NX * NY):
+    row = jnp.concatenate([mine, line], axis=1)
+    for k in range(sent_ref.shape[0]):
         sent_ref[k] = row
 
 
-def near_kernel(arrived_ref, sent_ref):
-    total = None
-    for x in range(NX):
-        line = None
-        for y in range(NY):
-            part = arrived_ref[x * NY + y][:, WIDE:]
-            line = part if line is None else line + part
-        if x:
-            line = pltpu.roll(line, x * PAIR * DOTS, 1)
-        total = line if total is None else total + line
-    for k in range(NZ * NC):
-        sent_ref[k] = total
-
-
-def last_kernel(far_ref, arrived_ref, iterate_ref, residual_ref, mapped_ref, lifted_ref, lifted_two_ref, new_iterate_ref, new_residual_ref):
-    core, x = lax.axis_index("c"), lax.axis_index("x")
-    totals = jnp.sum(far_ref[...], axis=0)
+def last_kernel(arrived_ref, iterate_ref, residual_ref, mapped_ref, lifted_ref, lifted_two_ref, new_iterate_ref, new_residual_ref):
+    core, x, low = lax.axis_index("c"), lax.axis_index("x"), lax.axis_index("zl")
+    group = NL * NC * NY
+    totals = None
+    for k in range(NX):
+        line = jnp.sum(arrived_ref[k * group : (k + 1) * group, :, WIDE:], axis=0)
+        if k:
+            line = pltpu.roll(line, k * PAIR * DOTS, 1)
+        totals = line if totals is None else totals + line
     lane = iota((SYS, LANE), 1)
     system = iota((SYS, LANE), 0)
     home = (system // PAIR) * (PAIR * DOTS) + (system % PAIR) * DOTS
@@ -215,7 +228,8 @@
     square_mid = square_map - 2.0 * alpha * mixed_map + alpha * alpha * square_two
     omega = cross_mid / square_mid
     mapped, lifted = mapped_ref[...], lifted_ref[...]
-    mapped_two = decoded([arrived_ref[p * NY + x][:, :WIDE] for p in range(SYS // PAIR)], core)
+    home = (low * NC + core) * NY + x
+    mapped_two = decoded([arrived_ref[p * group + home][:, :WIDE] for p in range(SYS // PAIR)], core)
     middle = residual_ref[...] - alpha * mapped
     lifted_mid = lifted - alpha * lifted_two_ref[...]
     new_iterate_ref[...] = iterate_ref[...] + alpha * lifted + omega * lifted_mid
@@ -231,7 +245,6 @@
         return jax.ShapeDtypeStruct(lengths, f32)
 
     hbm = pl.BlockSpec(memory_space=pltpu.HBM)
-    cut_shape = shape(NX * NC, NZ, 1, WIDE)
     small = shape(SYS, UNK)
     row = shape(1, WIDE)
     scratch = [
@@ -246,7 +259,7 @@
 
     cut, matrix, lifted, ride, residual, iterate = pl.pallas_call(
         first_kernel,
-        out_shape=(cut_shape, shape(UNK, UNK), small, shape(NX * NY, 1, WIDE), small, small),
+        out_shape=(shape(NX * NC, NZ, 1, WIDE), shape(UNK, UNK), small, shape(NX * NY, 1, WIDE), small, small),
         in_specs=[hbm] * 5,
         out_specs=[VM] * 6,
         scratch_shapes=scratch
@@ -259,17 +272,14 @@
         name="first_product",
     )(*inputs)
 
-    def reduced(cut):
-        near = exchanged(cut, ("x", "c")).sum(axis=0)
-        return exchanged(near, "z")
-
-    piece = reduced(cut).sum(axis=0)
+    near = exchanged(cut, ("x", "c")).sum(axis=0)
+    piece = exchanged(near, Z).sum(axis=0)
     sent = jnp.concatenate([jnp.broadcast_to(piece[None], ride.shape), ride], axis=2)
     arrived = exchanged(sent, ("x", "y"))
 
     cut, mapped, lifted_two, piece, other = pl.pallas_call(
         second_kernel,
-        out_shape=(cut_shape, small, small, row, row),
+        out_shape=(shape(NX * NL * NC, NH, 1, WIDE), small, small, row, row),
         in_specs=[VM, VM, hbm],
         out_specs=[VM] * 5,
         scratch_shapes=scratch,
@@ -277,38 +287,24 @@
         name="second_product",
     )(arrived, matrix, inputs[4])
 
-    sent = pl.pallas_call(
-        dots_kernel,
-        out_shape=shape(NX * NY, 1, WIDE + LANE),
-        in_specs=[VM] * 3,
-        out_specs=VM,
-        compiler_params=light,
-        name="dots",
-    )(reduced(cut), piece, other)
-    arrived = exchanged(sent, ("x", "y"))
-    sent = pl.pallas_call(
-        near_kernel,
-        out_shape=shape(NZ * NC, 1, LANE),
-        in_specs=[VM],
-        out_specs=VM,
-        compiler_params=light,
-        name="near_dots",
-    )(arrived)
-    far = exchanged(sent, ("z", "c"))
-    return tuple(
-        pl.pallas_call(
-            last_kernel,
-            out_shape=(small, small),
-            in_specs=[VM] * 7,
-            out_specs=[VM] * 2,
+    def call(kernel, name, out_shape, *operands):
+        return pl.pallas_call(
+            kernel,
+            out_shape=out_shape,
+            in_specs=[VM] * len(operands),
+            out_specs=jax.tree.map(lambda _: VM, out_shape),
             compiler_params=light,
-            name="update",
-        )(far, arrived, iterate, residual, mapped, lifted, lifted_two)
-    )
+            name=name,
+        )(*operands)
+
+    sent = call(share_kernel, "share", shape(NH, NH + 2, 1, WIDE), exchanged(cut, ("x", "zl", "c")), piece, other)
+    sent = call(dots_kernel, "dots", shape(NX * NL * NC * NY, 1, WIDE + LANE), exchanged(sent, "zh"))
+    arrived = exchanged(sent, ("x", "zl", "c", "y"))
+    return call(last_kernel, "update", (small, small), arrived, iterate, residual, mapped, lifted, lifted_two)
 
 
 def solution(mesh):
-    torus = Mesh(mesh.devices.reshape(NX, NZ, NC, NY), ("x", "z", "c", "y"))
+    torus = Mesh(mesh.devices.reshape(NX, NH, NL, NC, NY), (*ROWS, "y"))
     placed = (P(ROWS, "y"), P(ROWS, None, None), P(ROWS, None), P(None, ROWS), P(None, ROWS))
     return jax.shard_map(
         body, mesh=torus, in_specs=placed, out_specs=(P(None, ROWS), P(None, ROWS)), check_vma=False

time: 115 us -> 106 us (0.922)
  blocking collectives: 102 us -> 92.9 us
    all_to_all x7 -> x6, blocking collectives: 102 us -> 92.9 us  [exchanged(): return lax.all_to_all(pieces, axes, split_axis=0, concat_axis=0, tiled=True)]
where the time goes in v3:
time: 106 us
  blocking collectives  92.9 us (88%)
  Pallas kernels  12 us (11%)
    all_to_all x6, blocking collectives, exchanged(): return lax.all_to_all(pieces, axes, split_axis=0, concat_axis=0, tiled=True)  92.9 us
    pallas_call x1, Pallas kernels, body(): pl.pallas_call(first_kernel, out_shape=(shape(NX * NC, NZ, 1, WIDE), shap...  6.63 us
    pallas_call x1, Pallas kernels, body(): pl.pallas_call(second_kernel, out_shape=(shape(NX * NL * NC, NH, 1, WIDE)...  4.32 us

profile of v3, /device:TPU:1, one launch (start us, length us, event | category | flops | bytes accessed | tf_op | source)
XLA Modules:
  0.0 105.8 jit_solution(8193104476553635990)
XLA Ops:
  0.6 6.6 %first_product.1 = (f32[8,16,1,384]{3,2,1,0:T(1,128)S(1)}, f32[192,192]{1,0:T(8,128)S(1)}, f32[6,192]{1,0:T(8,128)S(1)}, f32[16,1,384]{2,1,0:T(1,128)S(1)}, f32[6,192]{1,0:T(8,128)S(1)}, /*index=5*/f32[6,192]{1,0:T(8,128)S(1)}) custom-call(s32[1,24]{1,0:T(1,128)} %len_hbm.1, f32[576,24]{1,0:T(8,128)} %bitcast.1, f32[6,192]{1,0:T(8,128)} %residual_hbm.1, ...), custom_call_target="tpu_custom_call" | custom-call | tf_op jit(solution)/shard_map/first_product/pallas_call | solution.py:260
  7.3 15.1 %all_to_all.30 = f32[8,16,1,384]{3,2,1,0:T(1,128)S(1)} all-to-all(f32[8,16,1,384]{3,2,1,0:T(1,128)S(1)} %get-tuple-element.13), channel_id=1, replica_groups=mesh['x'=4,'zh'=8,'zl'=2,'c'=2,'y'=4] {'x','c'}, dimensions={0} | all-to-all | bytes 393216 | tf_op jit(solution)/shard_map/all_to_all | solution.py:240
  22.4 0.1 reduce_sum.20
  22.5 22.5 %all_to_all.31 = f32[16,1,384]{2,1,0:T(1,128)S(1)} all-to-all(f32[16,1,384]{2,1,0:T(1,128)S(1)} %reduce_sum.21), channel_id=1, replica_groups=mesh['x'=4,'zh'=8,'zl'=2,'c'=2,'y'=4] {'zh','zl'}, dimensions={0} | all-to-all | bytes 49152 | tf_op jit(solution)/shard_map/all_to_all | solution.py:240
  45.1 11.2 %all_to_all.32.arrived_ref = f32[16,1,768]{2,1,0:T(1,128)S(1)} all-to-all(f32[16,1,768]{2,1,0:T(1,128)S(1)} %pad_maximum_fusion), channel_id=1, replica_groups=mesh['x'=4,'zh'=8,'zl'=2,'c'=2,'y'=4] {'x','y'}, dimensions={0} | all-to-all | bytes 98304 | tf_op jit(solution)/shard_map/all_to_all | solution.py:240
  56.3 4.3 %second_product.1 = (f32[16,8,1,384]{3,2,1,0:T(1,128)S(1)}, f32[6,192]{1,0:T(8,128)S(1)}, f32[6,192]{1,0:T(8,128)S(1)}, f32[1,384]{1,0:T(1,128)S(1)}, f32[1,384]{1,0:T(1,128)S(1)}) custom-call(f32[16,1,768]{2,1,0:T(1,128)S(1)} %all_to_all.32.arrived_ref, f32[192,192]{1,0:T(8,128)S(1)} %get-tuple-element.15.matrix_ref, f32[192,6144]{1,0:T(8,128)} %operator_hbm.3), custom_call_target="tpu_custom_call" | custom-call | tf_op jit(solution)/shard_map/second_product/pallas_call | solution.py:280
  60.6 12.9 %all_to_all.33.arrived_ref = f32[16,8,1,384]{3,2,1,0:T(1,128)S(1)} all-to-all(f32[16,8,1,384]{3,2,1,0:T(1,128)S(1)} %get-tuple-element.16), channel_id=1, replica_groups=mesh['x'=4,'zh'=8,'zl'=2,'c'=2,'y'=4] {'x','zl','c'}, dimensions={0} | all-to-all | bytes 393216 | tf_op jit(solution)/shard_map/all_to_all | solution.py:240
  73.5 0.1 share.1
  73.7 15.6 %all_to_all.34.far_ref = f32[8,10,1,384]{3,2,1,0:T(1,128)S(1)} all-to-all(f32[8,10,1,384]{3,2,1,0:T(1,128)S(1)} %share.1), channel_id=1, replica_groups=mesh['x'=4,'zh'=8,'zl'=2,'c'=2,'y'=4] {'zh'}, dimensions={0} | all-to-all | bytes 245760 | tf_op jit(solution)/shard_map/all_to_all | solution.py:240
  89.2 0.1 dots.1
  89.4 15.6 %all_to_all.35.arrived_ref = f32[64,1,512]{2,1,0:T(1,128)S(1)} all-to-all(f32[64,1,512]{2,1,0:T(1,128)S(1)} %dots.1), channel_id=1, replica_groups=mesh['x'=4,'zh'=8,'zl'=2,'c'=2,'y'=4] {'x','zl','c','y'}, dimensions={0} | all-to-all | bytes 262144 | tf_op jit(solution)/shard_map/all_to_all | solution.py:240
  105.0 0.8 update.1
  (4 shorter events, 0.1 us)

commit v4 on v3

--- a/solution.py
+++ b/solution.py
@@ -90,14 +90,10 @@
     ]
 
 
-def product(matrix, vector, copies, held, spread, cut_ref):
-    steps = cut_ref.shape[1]
-    inner = NZ // steps
+def product(matrix, vector, copies, held, spread, cut_ref, home):
     turned = nt(matrix, vector)
     for s in range(SYS):
         spread[s] = jnp.broadcast_to(turned[:, s : s + 1], (UNK, LANE))
-    for k in range(SYS // PAIR * inner * NC, NX * inner * NC):
-        cut_ref[k] = jnp.zeros((steps, 1, WIDE), f32)
     low = iota((1, LANE), 1) < REST
 
     def one(z, carry):
@@ -117,8 +113,7 @@
             hi = jnp.where(low, pltpu.roll(a[1], REST, 1), b[1])
             for c, row in ((0, (a[0], b[0], lo)), (1, (a[2], b[2], hi))):
                 for k in range(TILES):
-                    home = (p * inner + lax.rem(z, inner)) * NC + c
-                    cut_ref[home, lax.div(z, inner), :, k * LANE : (k + 1) * LANE] = row[k]
+                    cut_ref[*home(p, z, c), :, k * LANE : (k + 1) * LANE] = row[k]
         return carry
 
     per = NZ // COPIES
@@ -129,7 +124,7 @@
 
 def first_kernel(
     len_hbm, inverse_hbm, residual_hbm, iterate_hbm, operator_hbm,
-    cut_ref, matrix_ref, lifted_ref, ride_ref, residual_ref, iterate_ref,
+    cut_ref, matrix_ref, lifted_ref, residual_ref, iterate_ref,
     held, spread, sems, lengths, inverse, small_sems,
 ):
     small = [
@@ -145,41 +140,57 @@
         copy.start()
     for copy in small:
         copy.wait()
-    core = lax.axis_index("c")
     residual = residual_ref[...]
     matrix = preconditioner(lengths, inverse[...])
-    product(matrix, residual, copies, held, spread, cut_ref)
+    product(matrix, residual, copies, held, spread, cut_ref, lambda p, z, c: (z, c * (SYS // PAIR) + p))
     matrix_ref[...] = matrix
     lifted_ref[...] = nt(residual, matrix)
-    rows = encoded(residual, core)
-    for x in range(NX):
-        row = rows[x] if x < len(rows) else jnp.zeros((1, WIDE), f32)
-        for y in range(NY):
-            ride_ref[x * NY + y] = row
+
+
+def forward_kernel(arrived_ref, sent_ref):
+    rows = jnp.sum(arrived_ref[...], axis=0)
+    pairs = SYS // PAIR
+    for k in range(NX * NC * NY):
+        c = k // NY % NC
+        sent_ref[k] = rows[c * pairs : (c + 1) * pairs]
 
 
 def second_kernel(
-    arrived_ref, matrix_ref, operator_hbm, cut_ref, mapped_ref, lifted_ref, piece_ref, other_ref, held, spread, sems
+    arrived_ref, matrix_ref, residual_ref, operator_hbm, cut_ref, mapped_ref, lifted_ref, held, spread, sems
 ):
     copies = copies_of(operator_hbm, held, sems)
     for copy in copies:
         copy.start()
-    core, x, y = lax.axis_index("c"), lax.axis_index("x"), lax.axis_index("y")
-    mapped = decoded([arrived_ref[p * NY + x][:, :WIDE] for p in range(SYS // PAIR)], core)
+    core, x = lax.axis_index("c"), lax.axis_index("x")
+    total = None
+    for k in range(NX * NC):
+        part = arrived_ref[k * NY + x]
+        total = part if total is None else total + part
+    mapped = decoded([total[p] for p in range(SYS // PAIR)], core)
     matrix = matrix_ref[...]
-    product(matrix, mapped, copies, held, spread, cut_ref)
+    product(
+        matrix, mapped, copies, held, spread, cut_ref,
+        lambda p, z, c: ((p * NL + lax.rem(z, NL)) * NC + c, lax.div(z, NL)),
+    )
+    extra = [encoded(v, core) for v in (mapped, residual_ref[...])]
+    for k in range(NX * NL * NC):
+        p = k // (NL * NC)
+        if p < SYS // PAIR:
+            for e in range(len(extra)):
+                cut_ref[k, NH + e] = extra[e][p]
+        else:
+            cut_ref[k] = jnp.zeros((NH + 2, 1, WIDE), f32)
     mapped_ref[...] = mapped
     lifted_ref[...] = nt(mapped, matrix)
-    piece_ref[...] = arrived_ref[x * NY + y][:, :WIDE]
-    other_ref[...] = arrived_ref[y * NY][:, WIDE:]
-
-
-def share_kernel(arrived_ref, piece_ref, other_ref, sent_ref):
-    near = jnp.sum(arrived_ref[...], axis=0)
+
+
+def share_kernel(arrived_ref, sent_ref):
+    near = jnp.sum(arrived_ref[:, :NH], axis=0)
+    own = (lax.axis_index("y") * NL + lax.axis_index("zl")) * NC + lax.axis_index("c")
+    extra = arrived_ref[own, NH:]
     for k in range(NH):
         sent_ref[k, :NH] = near
-        sent_ref[k, NH] = piece_ref[...]
-        sent_ref[k, NH + 1] = other_ref[...]
+        sent_ref[k, NH:] = extra
 
 
 def dots_kernel(far_ref, sent_ref):
@@ -246,7 +257,6 @@
 
     hbm = pl.BlockSpec(memory_space=pltpu.HBM)
     small = shape(SYS, UNK)
-    row = shape(1, WIDE)
     scratch = [
         pltpu.VMEM(operator.shape, f32),
         pltpu.VMEM((SYS, UNK, LANE), f32),
@@ -257,11 +267,11 @@
     inputs = (block_len, block_inverse.reshape(BLOCKS * BLOCKS, BLOCKS), residual, iterate, operator)
     inputs = [pltpu.with_memory_space_constraint(a, pltpu.HBM) for a in inputs]
 
-    cut, matrix, lifted, ride, residual, iterate = pl.pallas_call(
+    cut, matrix, lifted, residual, iterate = pl.pallas_call(
         first_kernel,
-        out_shape=(shape(NX * NC, NZ, 1, WIDE), shape(UNK, UNK), small, shape(NX * NY, 1, WIDE), small, small),
+        out_shape=(shape(NZ, NC * SYS // PAIR, 1, WIDE), shape(UNK, UNK), small, small, small),
         in_specs=[hbm] * 5,
-        out_specs=[VM] * 6,
+        out_specs=[VM] * 5,
         scratch_shapes=scratch
         + [
             pltpu.SMEM((1, BLOCKS), jnp.int32),
@@ -272,21 +282,6 @@
         name="first_product",
     )(*inputs)
 
-    near = exchanged(cut, ("x", "c")).sum(axis=0)
-    piece = exchanged(near, Z).sum(axis=0)
-    sent = jnp.concatenate([jnp.broadcast_to(piece[None], ride.shape), ride], axis=2)
-    arrived = exchanged(sent, ("x", "y"))
-
-    cut, mapped, lifted_two, piece, other = pl.pallas_call(
-        second_kernel,
-        out_shape=(shape(NX * NL * NC, NH, 1, WIDE), small, small, row, row),
-        in_specs=[VM, VM, hbm],
-        out_specs=[VM] * 5,
-        scratch_shapes=scratch,
-        compiler_params=params,
-        name="second_product",
-    )(arrived, matrix, inputs[4])
-
     def call(kernel, name, out_shape, *operands):
         return pl.pallas_call(
             kernel,
@@ -297,7 +292,20 @@
             name=name,
         )(*operands)
 
-    sent = call(share_kernel, "share", shape(NH, NH + 2, 1, WIDE), exchanged(cut, ("x", "zl", "c")), piece, other)
+    sent = call(forward_kernel, "forward", shape(NX * NC * NY, SYS // PAIR, 1, WIDE), exchanged(cut, Z))
+    arrived = exchanged(sent, ("x", "c", "y"))
+
+    cut, mapped, lifted_two = pl.pallas_call(
+        second_kernel,
+        out_shape=(shape(NX * NL * NC, NH + 2, 1, WIDE), small, small),
+        in_specs=[VM, VM, VM, hbm],
+        out_specs=[VM] * 3,
+        scratch_shapes=scratch,
+        compiler_params=params,
+        name="second_product",
+    )(arrived, matrix, residual, inputs[4])
+
+    sent = call(share_kernel, "share", shape(NH, NH + 2, 1, WIDE), exchanged(cut, ("x", "zl", "c")))
     sent = call(dots_kernel, "dots", shape(NX * NL * NC * NY, 1, WIDE + LANE), exchanged(sent, "zh"))
     arrived = exchanged(sent, ("x", "zl", "c", "y"))
     return call(last_kernel, "update", (small, small), arrived, iterate, residual, mapped, lifted, lifted_two)

time: 106 us -> 102 us (0.962)
  blocking collectives: 92.9 us -> 89.3 us
    all_to_all x6 -> x5, blocking collectives: 92.9 us -> 89.3 us  [exchanged(): return lax.all_to_all(pieces, axes, split_axis=0, concat_axis=0, tiled=True)]
where the time goes in v4:
time: 102 us
  blocking collectives  89.3 us (88%)
  Pallas kernels  12.1 us (12%)
    all_to_all x5, blocking collectives, exchanged(): return lax.all_to_all(pieces, axes, split_axis=0, concat_axis=0, tiled=True)  89.3 us
    pallas_call x1, Pallas kernels, body(): pl.pallas_call(first_kernel, out_shape=(shape(NZ, NC * SYS // PAIR, 1, WI...  6.62 us
    pallas_call x1, Pallas kernels, body(): pl.pallas_call(second_kernel, out_shape=(shape(NX * NL * NC, NH + 2, 1, W...  4.33 us

profile of v4, /device:TPU:1, one launch (start us, length us, event | category | flops | bytes accessed | tf_op | source)
XLA Modules:
  0.0 102.1 jit_solution(9190599501386918099)
XLA Ops:
  0.6 6.6 %first_product.1 = (f32[16,6,1,384]{3,2,1,0:T(1,128)S(1)}, f32[192,192]{1,0:T(8,128)S(1)}, f32[6,192]{1,0:T(8,128)S(1)}, f32[6,192]{1,0:T(8,128)S(1)}, f32[6,192]{1,0:T(8,128)S(1)}) custom-call(s32[1,24]{1,0:T(1,128)} %len_hbm.1, f32[576,24]{1,0:T(8,128)} %bitcast.1, f32[6,192]{1,0:T(8,128)} %residual_hbm.1, f32[6,192]{1,0:T(8,128)} %iterate_hbm.1, ...), custom_call_target="tpu_custom_call" | custom-call | tf_op jit(solution)/shard_map/first_product/pallas_call | solution.py:270
  7.3 27.6 %all_to_all.25.arrived_ref = f32[16,6,1,384]{3,2,1,0:T(1,128)S(1)} all-to-all(f32[16,6,1,384]{3,2,1,0:T(1,128)S(1)} %get-tuple-element.10), channel_id=1, replica_groups=mesh['x'=4,'zh'=8,'zl'=2,'c'=2,'y'=4] {'zh','zl'}, dimensions={0} | all-to-all | bytes 294912 | tf_op jit(solution)/shard_map/all_to_all | solution.py:251
  34.8 0.1 forward.1
  35.0 18.6 %all_to_all.26.arrived_ref = f32[32,3,1,384]{3,2,1,0:T(1,128)S(1)} all-to-all(f32[32,3,1,384]{3,2,1,0:T(1,128)S(1)} %forward.1), channel_id=1, replica_groups=mesh['x'=4,'zh'=8,'zl'=2,'c'=2,'y'=4] {'x','c','y'}, dimensions={0} | all-to-all | bytes 294912 | tf_op jit(solution)/shard_map/all_to_all | solution.py:251
  53.6 4.3 %second_product.1 = (f32[16,10,1,384]{3,2,1,0:T(1,128)S(1)}, f32[6,192]{1,0:T(8,128)S(1)}, f32[6,192]{1,0:T(8,128)S(1)}) custom-call(f32[32,3,1,384]{3,2,1,0:T(1,128)S(1)} %all_to_all.26.arrived_ref, f32[192,192]{1,0:T(8,128)S(1)} %get-tuple-element.11.matrix_ref, f32[6,192]{1,0:T(8,128)S(1)} %get-tuple-element.12.residual_ref, f32[192,6144]{1,0:T(8,128)} %operator_hbm.3), custom_call_target="tpu_custom_call" | custom-call | tf_op jit(solution)/shard_map/second_product/pallas_call | solution.py:298
  57.9 10.8 %all_to_all.27.arrived_ref = f32[16,10,1,384]{3,2,1,0:T(1,128)S(1)} all-to-all(f32[16,10,1,384]{3,2,1,0:T(1,128)S(1)} %get-tuple-element.13), channel_id=1, replica_groups=mesh['x'=4,'zh'=8,'zl'=2,'c'=2,'y'=4] {'x','zl','c'}, dimensions={0} | all-to-all | bytes 491520 | tf_op jit(solution)/shard_map/all_to_all | solution.py:251
  68.8 0.1 share.1
  68.9 16.3 %all_to_all.28.far_ref = f32[8,10,1,384]{3,2,1,0:T(1,128)S(1)} all-to-all(f32[8,10,1,384]{3,2,1,0:T(1,128)S(1)} %share.1), channel_id=1, replica_groups=mesh['x'=4,'zh'=8,'zl'=2,'c'=2,'y'=4] {'zh'}, dimensions={0} | all-to-all | bytes 245760 | tf_op jit(solution)/shard_map/all_to_all | solution.py:251
  85.2 0.1 dots.1
  85.3 15.9 %all_to_all.29.arrived_ref = f32[64,1,512]{2,1,0:T(1,128)S(1)} all-to-all(f32[64,1,512]{2,1,0:T(1,128)S(1)} %dots.1), channel_id=1, replica_groups=mesh['x'=4,'zh'=8,'zl'=2,'c'=2,'y'=4] {'x','zl','c','y'}, dimensions={0} | all-to-all | bytes 262144 | tf_op jit(solution)/shard_map/all_to_all | solution.py:251
  101.3 0.8 update.1

commit v5 on v4

--- a/solution.py
+++ b/solution.py
@@ -19,10 +19,11 @@
 TILES = WIDE // LANE
 BLOCKS = 24
 COPIES = 4
+TOGETHER = 2
 DOTS = 6
 
 highest = lax.Precision.HIGHEST
-f32 = jnp.float32
+f32, bf16 = jnp.float32, jnp.bfloat16
 VM = pl.BlockSpec(memory_space=pltpu.VMEM)
 
 
@@ -32,6 +33,17 @@
 
 def nt(a, b):
     return lax.dot_general(a, b, (((1,), (1,)), ((), ())), precision=highest, preferred_element_type=f32)
+
+
+def split(value):
+    high = value.astype(bf16)
+    left = value - high.astype(f32)
+    middle = left.astype(bf16)
+    return high, middle, (left - middle.astype(f32)).astype(bf16)
+
+
+def one_pass(a, b):
+    return jnp.dot(a, b, preferred_element_type=f32)
 
 
 def preconditioner(len_ref, inverse):
@@ -52,10 +64,10 @@
         first = jnp.where(inside, start, first)
         last = jnp.where(inside, end, last)
         start = end
-    pick = (iota((UNK, slots), 0) == target).astype(f32)
-    rows = jnp.dot(pick, inverse, precision=highest, preferred_element_type=f32)
-    spread = (iota((BLOCKS, UNK), 0) == column - first).astype(f32)
-    full = jnp.dot(rows, spread, precision=highest, preferred_element_type=f32)
+    pick = (iota((UNK, slots), 0) == target).astype(f32).astype(bf16)
+    rows = sum(one_pass(pick, part) for part in split(inverse))
+    spread = (iota((BLOCKS, UNK), 0) == column - first).astype(f32).astype(bf16)
+    full = sum(one_pass(part, spread) for part in split(rows))
     row = iota((UNK, UNK), 0)
     return jnp.where((row >= first) & (row < last), full, 0.0)
 
@@ -82,44 +94,51 @@
 
 def copies_of(operator_ref, held, sems):
     width = operator_ref.shape[1] // COPIES
-    return [
-        pltpu.make_async_copy(
-            operator_ref.at[:, k * width : (k + 1) * width], held.at[:, k * width : (k + 1) * width], sems.at[k]
-        )
-        for k in range(COPIES)
-    ]
-
-
-def product(matrix, vector, copies, held, spread, cut_ref, home):
-    turned = nt(matrix, vector)
+
+    def copy_of(k):
+        columns = pl.ds(pl.multiple_of(k * width, LANE), width)
+        return pltpu.make_async_copy(operator_ref.at[:, columns], held.at[:, columns], sems.at[k])
+
+    return copy_of
+
+
+def product(matrix, vector, lifted_ref, copy_of, held, spread, cut_ref, home):
+    lifted = nt(vector, matrix)
+    lifted_ref[...] = lifted
+    turned = lifted.T
     for s in range(SYS):
         spread[s] = jnp.broadcast_to(turned[:, s : s + 1], (UNK, LANE))
     low = iota((1, LANE), 1) < REST
 
-    def one(z, carry):
-        base = pl.multiple_of(z * (NC * UNK), LANE)
-        totals = [[None] * TILES for _ in range(SYS)]
+    def one(step, carry):
+        totals = [[[None] * TILES for _ in range(SYS)] for _ in range(TOGETHER)]
+        base = pl.multiple_of(step * (TOGETHER * NC * UNK), LANE)
         for j in range(UNK // 8):
-            tiles = [held[8 * j : 8 * j + 8, pl.ds(base + k * LANE, LANE)] for k in range(TILES)]
             for s in range(SYS):
                 v = spread[s, 8 * j : 8 * j + 8, :]
-                for k in range(TILES):
-                    term = tiles[k] * v
-                    totals[s][k] = term if j == 0 else totals[s][k] + term
-        sums = [[jnp.sum(totals[s][k], axis=0, keepdims=True) for k in range(TILES)] for s in range(SYS)]
-        for p in range(SYS // PAIR):
-            a, b = sums[PAIR * p], sums[PAIR * p + 1]
-            lo = jnp.where(low, a[1], pltpu.roll(b[1], REST, 1))
-            hi = jnp.where(low, pltpu.roll(a[1], REST, 1), b[1])
-            for c, row in ((0, (a[0], b[0], lo)), (1, (a[2], b[2], hi))):
-                for k in range(TILES):
-                    cut_ref[*home(p, z, c), :, k * LANE : (k + 1) * LANE] = row[k]
+                for g in range(TOGETHER):
+                    for k in range(TILES):
+                        term = held[8 * j : 8 * j + 8, pl.ds(base + (g * TILES + k) * LANE, LANE)] * v
+                        totals[g][s][k] = term if j == 0 else totals[g][s][k] + term
+        for g in range(TOGETHER):
+            z = step * TOGETHER + g
+            sums = [[jnp.sum(totals[g][s][k], axis=0, keepdims=True) for k in range(TILES)] for s in range(SYS)]
+            for p in range(SYS // PAIR):
+                a, b = sums[PAIR * p], sums[PAIR * p + 1]
+                lo = jnp.where(low, a[1], pltpu.roll(b[1], REST, 1))
+                hi = jnp.where(low, pltpu.roll(a[1], REST, 1), b[1])
+                for c, row in ((0, (a[0], b[0], lo)), (1, (a[2], b[2], hi))):
+                    for k in range(TILES):
+                        cut_ref[*home(p, z, c), :, k * LANE : (k + 1) * LANE] = row[k]
         return carry
 
-    per = NZ // COPIES
-    for k in range(COPIES):
-        copies[k].wait()
-        lax.fori_loop(k * per, (k + 1) * per, one, 0)
+    per = NZ // COPIES // TOGETHER
+
+    def chunk(k, carry):
+        copy_of(k).wait()
+        return lax.fori_loop(k * per, (k + 1) * per, one, carry)
+
+    lax.fori_loop(0, COPIES, chunk, 0)
 
 
 def first_kernel(
@@ -135,16 +154,16 @@
     ]
     for copy in small:
         copy.start()
-    copies = copies_of(operator_hbm, held, sems)
-    for copy in copies:
-        copy.start()
+    copy_of = copies_of(operator_hbm, held, sems)
+    copy_of(0).start()
     for copy in small:
         copy.wait()
+    for k in range(1, COPIES):
+        copy_of(k).start()
     residual = residual_ref[...]
     matrix = preconditioner(lengths, inverse[...])
-    product(matrix, residual, copies, held, spread, cut_ref, lambda p, z, c: (z, c * (SYS // PAIR) + p))
+    product(matrix, residual, lifted_ref, copy_of, held, spread, cut_ref, lambda p, z, c: (z, c * (SYS // PAIR) + p))
     matrix_ref[...] = matrix
-    lifted_ref[...] = nt(residual, matrix)
 
 
 def forward_kernel(arrived_ref, sent_ref):
@@ -158,9 +177,9 @@
 def second_kernel(
     arrived_ref, matrix_ref, residual_ref, operator_hbm, cut_ref, mapped_ref, lifted_ref, held, spread, sems
 ):
-    copies = copies_of(operator_hbm, held, sems)
-    for copy in copies:
-        copy.start()
+    copy_of = copies_of(operator_hbm, held, sems)
+    for k in range(COPIES):
+        copy_of(k).start()
     core, x = lax.axis_index("c"), lax.axis_index("x")
     total = None
     for k in range(NX * NC):
@@ -169,7 +188,7 @@
     mapped = decoded([total[p] for p in range(SYS // PAIR)], core)
     matrix = matrix_ref[...]
     product(
-        matrix, mapped, copies, held, spread, cut_ref,
+        matrix, mapped, lifted_ref, copy_of, held, spread, cut_ref,
         lambda p, z, c: ((p * NL + lax.rem(z, NL)) * NC + c, lax.div(z, NL)),
     )
     extra = [encoded(v, core) for v in (mapped, residual_ref[...])]
@@ -181,7 +200,6 @@
         else:
             cut_ref[k] = jnp.zeros((NH + 2, 1, WIDE), f32)
     mapped_ref[...] = mapped
-    lifted_ref[...] = nt(mapped, matrix)
 
 
 def share_kernel(arrived_ref, sent_ref):

time: 102 us -> 100 us (0.980)
  Pallas kernels: 12.1 us -> 9.98 us
    pallas_call x1, Pallas kernels: 6.62 us -> 4.81 us  [body(): pl.pallas_call(first_kernel, out_shape=(shape(NZ, NC * SYS // PAIR, 1, WI...]
where the time goes in v5:
time: 100 us; the launch traced here: 99.9 us
  blocking collectives  89.3 us (89%)
  Pallas kernels  9.98 us (10%)
    all_to_all x5, blocking collectives, exchanged(): return lax.all_to_all(pieces, axes, split_axis=0, concat_axis=0, tiled=True)  89.3 us
    pallas_call x1, Pallas kernels, body(): pl.pallas_call(first_kernel, out_shape=(shape(NZ, NC * SYS // PAIR, 1, WI...  4.81 us
    pallas_call x1, Pallas kernels, body(): pl.pallas_call(second_kernel, out_shape=(shape(NX * NL * NC, NH + 2, 1, W...  3.99 us

profile of v5, /device:TPU:1, one launch (start us, length us, event | category | flops | bytes accessed | tf_op | source)
XLA Modules:
  0.0 99.9 jit_solution(13241540778247950159)
XLA Ops:
  0.6 4.8 %first_product.1 = (f32[16,6,1,384]{3,2,1,0:T(1,128)S(1)}, f32[192,192]{1,0:T(8,128)S(1)}, f32[6,192]{1,0:T(8,128)S(1)}, f32[6,192]{1,0:T(8,128)S(1)}, f32[6,192]{1,0:T(8,128)S(1)}) custom-call(s32[1,24]{1,0:T(1,128)} %len_hbm.1, f32[576,24]{1,0:T(8,128)} %bitcast.1, f32[6,192]{1,0:T(8,128)} %residual_hbm.1, f32[6,192]{1,0:T(8,128)} %iterate_hbm.1, ...), custom_call_target="tpu_custom_call" | custom-call | tf_op jit(solution)/shard_map/first_product/pallas_call | solution.py:288
  5.5 27.6 %all_to_all.25.arrived_ref = f32[16,6,1,384]{3,2,1,0:T(1,128)S(1)} all-to-all(f32[16,6,1,384]{3,2,1,0:T(1,128)S(1)} %get-tuple-element.10), channel_id=1, replica_groups=mesh['x'=4,'zh'=8,'zl'=2,'c'=2,'y'=4] {'zh','zl'}, dimensions={0} | all-to-all | bytes 294912 | tf_op jit(solution)/shard_map/all_to_all | solution.py:269
  33.0 0.1 forward.1
  33.1 18.6 %all_to_all.26.arrived_ref = f32[32,3,1,384]{3,2,1,0:T(1,128)S(1)} all-to-all(f32[32,3,1,384]{3,2,1,0:T(1,128)S(1)} %forward.1), channel_id=1, replica_groups=mesh['x'=4,'zh'=8,'zl'=2,'c'=2,'y'=4] {'x','c','y'}, dimensions={0} | all-to-all | bytes 294912 | tf_op jit(solution)/shard_map/all_to_all | solution.py:269
  51.8 4.0 %second_product.1 = (f32[16,10,1,384]{3,2,1,0:T(1,128)S(1)}, f32[6,192]{1,0:T(8,128)S(1)}, f32[6,192]{1,0:T(8,128)S(1)}) custom-call(f32[32,3,1,384]{3,2,1,0:T(1,128)S(1)} %all_to_all.26.arrived_ref, f32[192,192]{1,0:T(8,128)S(1)} %get-tuple-element.11.matrix_ref, f32[6,192]{1,0:T(8,128)S(1)} %get-tuple-element.12.residual_ref, f32[192,6144]{1,0:T(8,128)} %operator_hbm.3), custom_call_target="tpu_custom_call" | custom-call | tf_op jit(solution)/shard_map/second_product/pallas_call | solution.py:316
  55.8 10.8 %all_to_all.27.arrived_ref = f32[16,10,1,384]{3,2,1,0:T(1,128)S(1)} all-to-all(f32[16,10,1,384]{3,2,1,0:T(1,128)S(1)} %get-tuple-element.13), channel_id=1, replica_groups=mesh['x'=4,'zh'=8,'zl'=2,'c'=2,'y'=4] {'x','zl','c'}, dimensions={0} | all-to-all | bytes 491520 | tf_op jit(solution)/shard_map/all_to_all | solution.py:269
  66.6 0.1 share.1
  66.8 16.3 %all_to_all.28.far_ref = f32[8,10,1,384]{3,2,1,0:T(1,128)S(1)} all-to-all(f32[8,10,1,384]{3,2,1,0:T(1,128)S(1)} %share.1), channel_id=1, replica_groups=mesh['x'=4,'zh'=8,'zl'=2,'c'=2,'y'=4] {'zh'}, dimensions={0} | all-to-all | bytes 245760 | tf_op jit(solution)/shard_map/all_to_all | solution.py:269
  83.1 0.1 dots.1
  83.2 15.9 %all_to_all.29.arrived_ref = f32[64,1,512]{2,1,0:T(1,128)S(1)} all-to-all(f32[64,1,512]{2,1,0:T(1,128)S(1)} %dots.1), channel_id=1, replica_groups=mesh['x'=4,'zh'=8,'zl'=2,'c'=2,'y'=4] {'x','zl','c','y'}, dimensions={0} | all-to-all | bytes 262144 | tf_op jit(solution)/shard_map/all_to_all | solution.py:269
  99.1 0.8 update.1

commit v6 on v5

--- a/solution.py
+++ b/solution.py
@@ -21,6 +21,8 @@
 COPIES = 4
 TOGETHER = 2
 DOTS = 6
+PAIRS = SYS // PAIR
+EACH = PAIRS * NH // NX
 
 highest = lax.Precision.HIGHEST
 f32, bf16 = jnp.float32, jnp.bfloat16
@@ -76,7 +78,7 @@
     main = jnp.where(core == 0, vector[:, :LANE], vector[:, REST:])
     rest = jnp.where(core == 0, vector[:, LANE:], vector[:, :REST])
     rows = []
-    for p in range(SYS // PAIR):
+    for p in range(PAIRS):
         a, b = PAIR * p, PAIR * p + 1
         rows.append(jnp.concatenate([main[a : a + 1], main[b : b + 1], rest[a : a + 1], rest[b : b + 1]], axis=1))
     return rows
@@ -123,7 +125,7 @@
         for g in range(TOGETHER):
             z = step * TOGETHER + g
             sums = [[jnp.sum(totals[g][s][k], axis=0, keepdims=True) for k in range(TILES)] for s in range(SYS)]
-            for p in range(SYS // PAIR):
+            for p in range(PAIRS):
                 a, b = sums[PAIR * p], sums[PAIR * p + 1]
                 lo = jnp.where(low, a[1], pltpu.roll(b[1], REST, 1))
                 hi = jnp.where(low, pltpu.roll(a[1], REST, 1), b[1])
@@ -162,13 +164,13 @@
         copy_of(k).start()
     residual = residual_ref[...]
     matrix = preconditioner(lengths, inverse[...])
-    product(matrix, residual, lifted_ref, copy_of, held, spread, cut_ref, lambda p, z, c: (z, c * (SYS // PAIR) + p))
+    product(matrix, residual, lifted_ref, copy_of, held, spread, cut_ref, lambda p, z, c: (z, c * (PAIRS) + p))
     matrix_ref[...] = matrix
 
 
 def forward_kernel(arrived_ref, sent_ref):
     rows = jnp.sum(arrived_ref[...], axis=0)
-    pairs = SYS // PAIR
+    pairs = PAIRS
     for k in range(NX * NC * NY):
         c = k // NY % NC
         sent_ref[k] = rows[c * pairs : (c + 1) * pairs]
@@ -185,67 +187,73 @@
     for k in range(NX * NC):
         part = arrived_ref[k * NY + x]
         total = part if total is None else total + part
-    mapped = decoded([total[p] for p in range(SYS // PAIR)], core)
+    mapped = decoded([total[p] for p in range(PAIRS)], core)
     matrix = matrix_ref[...]
-    product(
-        matrix, mapped, lifted_ref, copy_of, held, spread, cut_ref,
-        lambda p, z, c: ((p * NL + lax.rem(z, NL)) * NC + c, lax.div(z, NL)),
-    )
-    extra = [encoded(v, core) for v in (mapped, residual_ref[...])]
-    for k in range(NX * NL * NC):
-        p = k // (NL * NC)
-        if p < SYS // PAIR:
-            for e in range(len(extra)):
-                cut_ref[k, NH + e] = extra[e][p]
-        else:
-            cut_ref[k] = jnp.zeros((NH + 2, 1, WIDE), f32)
+
+    def home(p, z, c):
+        row = p * NH + lax.div(z, NL)
+        x = lax.div(row, EACH)
+        return (x * NL + lax.rem(z, NL)) * NC + c, row - x * EACH
+
+    product(matrix, mapped, lifted_ref, copy_of, held, spread, cut_ref, home)
+    step = lax.axis_index("zh")
+    for e, vector in enumerate((mapped, residual_ref[...])):
+        extra = encoded(vector, core)
+        for to in range(NX):
+            row = jnp.zeros((1, WIDE), f32)
+            for p in range(PAIRS):
+                at = p * NH + step - to * EACH
+                row = jnp.where((at >= 0) & (at < EACH), extra[p], row)
+            for k in range(NL * NC):
+                cut_ref[to * NL * NC + k, EACH + e] = row
     mapped_ref[...] = mapped
 
 
 def share_kernel(arrived_ref, sent_ref):
-    near = jnp.sum(arrived_ref[:, :NH], axis=0)
+    near = jnp.sum(arrived_ref[:, :EACH], axis=0)
     own = (lax.axis_index("y") * NL + lax.axis_index("zl")) * NC + lax.axis_index("c")
-    extra = arrived_ref[own, NH:]
+    extra = arrived_ref[own, EACH:]
     for k in range(NH):
-        sent_ref[k, :NH] = near
-        sent_ref[k, NH:] = extra
+        sent_ref[k, :EACH] = near
+        sent_ref[k, EACH:] = extra
 
 
 def dots_kernel(far_ref, sent_ref):
-    mine = far_ref[0, lax.axis_index("zh")]
-    for k in range(1, NH):
-        mine = mine + far_ref[k, lax.axis_index("zh")]
-    terms = [None] * DOTS
-    for h in range(NH):
-        t = far_ref[0, h]
+    base = lax.axis_index("x") * EACH
+    first = lax.div(base, NH)
+    step = lax.axis_index("zh")
+    mine = jnp.zeros((1, WIDE), f32)
+    terms = [jnp.zeros((1, WIDE), f32)] * (2 * DOTS)
+    for j in range(EACH):
+        t = far_ref[0, j]
         for k in range(1, NH):
-            t = t + far_ref[k, h]
-        m, r = far_ref[h, NH], far_ref[h, NH + 1]
+            t = t + far_ref[k, j]
+        h = lax.rem(base + j, NH)
+        mine = jnp.where(h == step, t, mine)
+        m, r = far_ref[h, EACH], far_ref[h, EACH + 1]
+        same = lax.div(base + j, NH) == first
         for d, term in enumerate((r * r, r * m, m * m, t * r, t * m, t * t)):
-            terms[d] = term if h == 0 else terms[d] + term
+            terms[d] = terms[d] + jnp.where(same, term, 0.0)
+            terms[DOTS + d] = terms[DOTS + d] + jnp.where(same, 0.0, term)
     terms = jnp.concatenate(terms, axis=0)
-    shared = terms[:, PAIR * LANE :]
+    main, other, shared = (terms[:, k * LANE : (k + 1) * LANE] for k in range(TILES))
     low = iota(shared.shape, 1) < REST
-    sides = jnp.concatenate(
-        [terms[:, :LANE] + jnp.where(low, shared, 0.0), terms[:, LANE : 2 * LANE] + jnp.where(low, 0.0, shared)], axis=0
-    )
-    column = jnp.sum(sides, axis=1, keepdims=True)
-    shape = (PAIR * DOTS, LANE)
-    line = jnp.sum(jnp.where(iota(shape, 0) == iota(shape, 1), column, 0.0), axis=0, keepdims=True)
+    main = main + jnp.where(low, shared, 0.0)
+    other = other + jnp.where(low, 0.0, shared)
+    column = jnp.sum(
+        jnp.concatenate([main[:DOTS], other[:DOTS], main[DOTS:], other[DOTS:]], axis=0), axis=1, keepdims=True
+    )
+    shape = (2 * PAIR * DOTS, LANE)
+    place = iota(shape, 0) + first * (PAIR * DOTS)
+    line = jnp.sum(jnp.where(place == iota(shape, 1), column, 0.0), axis=0, keepdims=True)
     row = jnp.concatenate([mine, line], axis=1)
     for k in range(sent_ref.shape[0]):
         sent_ref[k] = row
 
 
 def last_kernel(arrived_ref, iterate_ref, residual_ref, mapped_ref, lifted_ref, lifted_two_ref, new_iterate_ref, new_residual_ref):
-    core, x, low = lax.axis_index("c"), lax.axis_index("x"), lax.axis_index("zl")
-    group = NL * NC * NY
-    totals = None
-    for k in range(NX):
-        line = jnp.sum(arrived_ref[k * group : (k + 1) * group, :, WIDE:], axis=0)
-        if k:
-            line = pltpu.roll(line, k * PAIR * DOTS, 1)
-        totals = line if totals is None else totals + line
+    core, x = lax.axis_index("c"), lax.axis_index("x")
+    totals = jnp.sum(arrived_ref[:, :, WIDE:], axis=0)
     lane = iota((SYS, LANE), 1)
     system = iota((SYS, LANE), 0)
     home = (system // PAIR) * (PAIR * DOTS) + (system % PAIR) * DOTS
@@ -257,8 +265,11 @@
     square_mid = square_map - 2.0 * alpha * mixed_map + alpha * alpha * square_two
     omega = cross_mid / square_mid
     mapped, lifted = mapped_ref[...], lifted_ref[...]
-    home = (low * NC + core) * NY + x
-    mapped_two = decoded([arrived_ref[p * group + home][:, :WIDE] for p in range(SYS // PAIR)], core)
+    rows = []
+    for p in range(PAIRS):
+        source = lax.div(p * NH + lax.axis_index("zh"), EACH)
+        rows.append(arrived_ref[((source * NL + lax.axis_index("zl")) * NC + core) * NY + x][:, :WIDE])
+    mapped_two = decoded(rows, core)
     middle = residual_ref[...] - alpha * mapped
     lifted_mid = lifted - alpha * lifted_two_ref[...]
     new_iterate_ref[...] = iterate_ref[...] + alpha * lifted + omega * lifted_mid
@@ -287,7 +298,7 @@
 
     cut, matrix, lifted, residual, iterate = pl.pallas_call(
         first_kernel,
-        out_shape=(shape(NZ, NC * SYS // PAIR, 1, WIDE), shape(UNK, UNK), small, small, small),
+        out_shape=(shape(NZ, NC * PAIRS, 1, WIDE), shape(UNK, UNK), small, small, small),
         in_specs=[hbm] * 5,
         out_specs=[VM] * 5,
         scratch_shapes=scratch
@@ -310,12 +321,12 @@
             name=name,
         )(*operands)
 
-    sent = call(forward_kernel, "forward", shape(NX * NC * NY, SYS // PAIR, 1, WIDE), exchanged(cut, Z))
+    sent = call(forward_kernel, "forward", shape(NX * NC * NY, PAIRS, 1, WIDE), exchanged(cut, Z))
     arrived = exchanged(sent, ("x", "c", "y"))
 
     cut, mapped, lifted_two = pl.pallas_call(
         second_kernel,
-        out_shape=(shape(NX * NL * NC, NH + 2, 1, WIDE), small, small),
+        out_shape=(shape(NX * NL * NC, EACH + 2, 1, WIDE), small, small),
         in_specs=[VM, VM, VM, hbm],
         out_specs=[VM] * 3,
         scratch_shapes=scratch,
@@ -323,7 +334,7 @@
         name="second_product",
     )(arrived, matrix, residual, inputs[4])
 
-    sent = call(share_kernel, "share", shape(NH, NH + 2, 1, WIDE), exchanged(cut, ("x", "zl", "c")))
+    sent = call(share_kernel, "share", shape(NH, EACH + 2, 1, WIDE), exchanged(cut, ("x", "zl", "c")))
     sent = call(dots_kernel, "dots", shape(NX * NL * NC * NY, 1, WIDE + LANE), exchanged(sent, "zh"))
     arrived = exchanged(sent, ("x", "zl", "c", "y"))
     return call(last_kernel, "update", (small, small), arrived, iterate, residual, mapped, lifted, lifted_two)

time: 100 us -> 98.9 us (0.989)
  blocking collectives: 89.3 us -> 88 us
    all_to_all x5, blocking collectives: 89.3 us -> 88 us  [exchanged(): return lax.all_to_all(pieces, axes, split_axis=0, concat_axis=0, tiled=True)]
where the time goes in v6:
time: 98.9 us; the launch traced here: 98.6 us
  blocking collectives  88 us (89%)
  Pallas kernels  9.98 us (10%)
    all_to_all x5, blocking collectives, exchanged(): return lax.all_to_all(pieces, axes, split_axis=0, concat_axis=0, tiled=True)  88 us
    pallas_call x1, Pallas kernels, body(): pl.pallas_call(first_kernel, out_shape=(shape(NZ, NC * PAIRS, 1, WIDE), s...  4.81 us
    pallas_call x1, Pallas kernels, body(): pl.pallas_call(second_kernel, out_shape=(shape(NX * NL * NC, EACH + 2, 1,...  4.01 us

profile of v6, /device:TPU:1, one launch (start us, length us, event | category | flops | bytes accessed | tf_op | source)
XLA Modules:
  0.0 98.6 jit_solution(14929248030278524324)
XLA Ops:
  0.6 4.8 %first_product.1 = (f32[16,6,1,384]{3,2,1,0:T(1,128)S(1)}, f32[192,192]{1,0:T(8,128)S(1)}, f32[6,192]{1,0:T(8,128)S(1)}, f32[6,192]{1,0:T(8,128)S(1)}, f32[6,192]{1,0:T(8,128)S(1)}) custom-call(s32[1,24]{1,0:T(1,128)} %len_hbm.1, f32[576,24]{1,0:T(8,128)} %bitcast.1, f32[6,192]{1,0:T(8,128)} %residual_hbm.1, f32[6,192]{1,0:T(8,128)} %iterate_hbm.1, ...), custom_call_target="tpu_custom_call" | custom-call | tf_op jit(solution)/shard_map/first_product/pallas_call | solution.py:299
  5.5 27.6 %all_to_all.25.arrived_ref = f32[16,6,1,384]{3,2,1,0:T(1,128)S(1)} all-to-all(f32[16,6,1,384]{3,2,1,0:T(1,128)S(1)} %get-tuple-element.10), channel_id=1, replica_groups=mesh['x'=4,'zh'=8,'zl'=2,'c'=2,'y'=4] {'zh','zl'}, dimensions={0} | all-to-all | bytes 294912 | tf_op jit(solution)/shard_map/all_to_all | solution.py:280
  33.0 0.1 forward.1
  33.1 18.6 %all_to_all.26.arrived_ref = f32[32,3,1,384]{3,2,1,0:T(1,128)S(1)} all-to-all(f32[32,3,1,384]{3,2,1,0:T(1,128)S(1)} %forward.1), channel_id=1, replica_groups=mesh['x'=4,'zh'=8,'zl'=2,'c'=2,'y'=4] {'x','c','y'}, dimensions={0} | all-to-all | bytes 294912 | tf_op jit(solution)/shard_map/all_to_all | solution.py:280
  51.8 4.0 %second_product.1 = (f32[16,8,1,384]{3,2,1,0:T(1,128)S(1)}, f32[6,192]{1,0:T(8,128)S(1)}, f32[6,192]{1,0:T(8,128)S(1)}) custom-call(f32[32,3,1,384]{3,2,1,0:T(1,128)S(1)} %all_to_all.26.arrived_ref, f32[192,192]{1,0:T(8,128)S(1)} %get-tuple-element.11.matrix_ref, f32[6,192]{1,0:T(8,128)S(1)} %get-tuple-element.12.residual_ref, f32[192,6144]{1,0:T(8,128)} %operator_hbm.3), custom_call_target="tpu_custom_call" | custom-call | tf_op jit(solution)/shard_map/second_product/pallas_call | solution.py:327
  55.8 10.4 %all_to_all.27.arrived_ref = f32[16,8,1,384]{3,2,1,0:T(1,128)S(1)} all-to-all(f32[16,8,1,384]{3,2,1,0:T(1,128)S(1)} %get-tuple-element.13), channel_id=1, replica_groups=mesh['x'=4,'zh'=8,'zl'=2,'c'=2,'y'=4] {'x','zl','c'}, dimensions={0} | all-to-all | bytes 393216 | tf_op jit(solution)/shard_map/all_to_all | solution.py:280
  66.2 0.1 share.1
  66.3 16.1 %all_to_all.28.far_ref = f32[8,8,1,384]{3,2,1,0:T(1,128)S(1)} all-to-all(f32[8,8,1,384]{3,2,1,0:T(1,128)S(1)} %share.1), channel_id=1, replica_groups=mesh['x'=4,'zh'=8,'zl'=2,'c'=2,'y'=4] {'zh'}, dimensions={0} | all-to-all | bytes 196608 | tf_op jit(solution)/shard_map/all_to_all | solution.py:280
  82.5 0.2 dots.1
  82.6 15.2 %all_to_all.29.arrived_ref = f32[64,1,512]{2,1,0:T(1,128)S(1)} all-to-all(f32[64,1,512]{2,1,0:T(1,128)S(1)} %dots.1), channel_id=1, replica_groups=mesh['x'=4,'zh'=8,'zl'=2,'c'=2,'y'=4] {'x','zl','c','y'}, dimensions={0} | all-to-all | bytes 262144 | tf_op jit(solution)/shard_map/all_to_all | solution.py:280
  97.8 0.8 update.1

commit v7 on v6

--- a/solution.py
+++ b/solution.py
@@ -134,6 +134,9 @@
                         cut_ref[*home(p, z, c), :, k * LANE : (k + 1) * LANE] = row[k]
         return carry
 
+    if copy_of is None:
+        lax.fori_loop(0, NZ // TOGETHER, one, 0)
+        return
     per = NZ // COPIES // TOGETHER
 
     def chunk(k, carry):
@@ -145,8 +148,8 @@
 
 def first_kernel(
     len_hbm, inverse_hbm, residual_hbm, iterate_hbm, operator_hbm,
-    cut_ref, matrix_ref, lifted_ref, residual_ref, iterate_ref,
-    held, spread, sems, lengths, inverse, small_sems,
+    cut_ref, matrix_ref, lifted_ref, residual_ref, iterate_ref, held,
+    spread, sems, lengths, inverse, small_sems,
 ):
     small = [
         pltpu.make_async_copy(source, target, small_sems.at[k])
@@ -177,11 +180,8 @@
 
 
 def second_kernel(
-    arrived_ref, matrix_ref, residual_ref, operator_hbm, cut_ref, mapped_ref, lifted_ref, held, spread, sems
+    arrived_ref, matrix_ref, residual_ref, held, cut_ref, mapped_ref, lifted_ref, spread
 ):
-    copy_of = copies_of(operator_hbm, held, sems)
-    for k in range(COPIES):
-        copy_of(k).start()
     core, x = lax.axis_index("c"), lax.axis_index("x")
     total = None
     for k in range(NX * NC):
@@ -195,7 +195,7 @@
         x = lax.div(row, EACH)
         return (x * NL + lax.rem(z, NL)) * NC + c, row - x * EACH
 
-    product(matrix, mapped, lifted_ref, copy_of, held, spread, cut_ref, home)
+    product(matrix, mapped, lifted_ref, None, held, spread, cut_ref, home)
     step = lax.axis_index("zh")
     for e, vector in enumerate((mapped, residual_ref[...])):
         extra = encoded(vector, core)
@@ -286,23 +286,20 @@
 
     hbm = pl.BlockSpec(memory_space=pltpu.HBM)
     small = shape(SYS, UNK)
-    scratch = [
-        pltpu.VMEM(operator.shape, f32),
-        pltpu.VMEM((SYS, UNK, LANE), f32),
-        pltpu.SemaphoreType.DMA((COPIES,)),
-    ]
+    scratch = [pltpu.VMEM((SYS, UNK, LANE), f32)]
     params = pltpu.CompilerParams(vmem_limit_bytes=16 << 20)
     light = pltpu.CompilerParams(vmem_limit_bytes=4 << 20)
     inputs = (block_len, block_inverse.reshape(BLOCKS * BLOCKS, BLOCKS), residual, iterate, operator)
     inputs = [pltpu.with_memory_space_constraint(a, pltpu.HBM) for a in inputs]
 
-    cut, matrix, lifted, residual, iterate = pl.pallas_call(
+    cut, matrix, lifted, residual, iterate, held = pl.pallas_call(
         first_kernel,
-        out_shape=(shape(NZ, NC * PAIRS, 1, WIDE), shape(UNK, UNK), small, small, small),
+        out_shape=(shape(NZ, NC * PAIRS, 1, WIDE), shape(UNK, UNK), small, small, small, shape(*operator.shape)),
         in_specs=[hbm] * 5,
-        out_specs=[VM] * 5,
-        scratch_shapes=scratch
-        + [
+        out_specs=[VM] * 6,
+        scratch_shapes=[
+            *scratch,
+            pltpu.SemaphoreType.DMA((COPIES,)),
             pltpu.SMEM((1, BLOCKS), jnp.int32),
             pltpu.VMEM((BLOCKS * BLOCKS, BLOCKS), f32),
             pltpu.SemaphoreType.DMA((4,)),
@@ -327,12 +324,12 @@
     cut, mapped, lifted_two = pl.pallas_call(
         second_kernel,
         out_shape=(shape(NX * NL * NC, EACH + 2, 1, WIDE), small, small),
-        in_specs=[VM, VM, VM, hbm],
+        in_specs=[VM] * 4,
         out_specs=[VM] * 3,
         scratch_shapes=scratch,
         compiler_params=params,
         name="second_product",
-    )(arrived, matrix, residual, inputs[4])
+    )(arrived, matrix, residual, held)
 
     sent = call(share_kernel, "share", shape(NH, EACH + 2, 1, WIDE), exchanged(cut, ("x", "zl", "c")))
     sent = call(dots_kernel, "dots", shape(NX * NL * NC * NY, 1, WIDE + LANE), exchanged(sent, "zh"))

time: 98.9 us -> 97.9 us (0.990)
  no operation moved by 1% of the time
where the time goes in v7:
time: 97.9 us; the launch traced here: 97.6 us
  blocking collectives  88 us (90%)
  Pallas kernels  9.01 us (9%)
    all_to_all x5, blocking collectives, exchanged(): return lax.all_to_all(pieces, axes, split_axis=0, concat_axis=0, tiled=True)  88 us
    pallas_call x1, Pallas kernels, body(): pl.pallas_call(first_kernel, out_shape=(shape(NZ, NC * PAIRS, 1, WIDE), s...  4.81 us
    pallas_call x1, Pallas kernels, body(): pl.pallas_call(second_kernel, out_shape=(shape(NX * NL * NC, EACH + 2, 1,...  3.04 us

profile of v7, /device:TPU:1, one launch (start us, length us, event | category | flops | bytes accessed | tf_op | source)
XLA Modules:
  0.0 97.6 jit_solution(18422397997153278405)
XLA Ops:
  0.6 4.8 %first_product.1 = (f32[16,6,1,384]{3,2,1,0:T(1,128)S(1)}, f32[192,192]{1,0:T(8,128)S(1)}, f32[6,192]{1,0:T(8,128)S(1)}, f32[6,192]{1,0:T(8,128)S(1)}, f32[6,192]{1,0:T(8,128)S(1)}, /*index=5*/f32[192,6144]{1,0:T(8,128)S(1)}) custom-call(s32[1,24]{1,0:T(1,128)} %len_hbm.1, f32[576,24]{1,0:T(8,128)} %bitcast.1, f32[6,192]{1,0:T(8,128)} %residual_hbm.1, ...), custom_call_target="tpu_custom_call" | custom-call | tf_op jit(solution)/shard_map/first_product/pallas_call | solution.py:295
  5.5 27.6 %all_to_all.25.arrived_ref = f32[16,6,1,384]{3,2,1,0:T(1,128)S(1)} all-to-all(f32[16,6,1,384]{3,2,1,0:T(1,128)S(1)} %get-tuple-element.11), channel_id=1, replica_groups=mesh['x'=4,'zh'=8,'zl'=2,'c'=2,'y'=4] {'zh','zl'}, dimensions={0} | all-to-all | bytes 294912 | tf_op jit(solution)/shard_map/all_to_all | solution.py:280
  33.0 0.1 forward.1
  33.2 18.6 %all_to_all.26.arrived_ref = f32[32,3,1,384]{3,2,1,0:T(1,128)S(1)} all-to-all(f32[32,3,1,384]{3,2,1,0:T(1,128)S(1)} %forward.1), channel_id=1, replica_groups=mesh['x'=4,'zh'=8,'zl'=2,'c'=2,'y'=4] {'x','c','y'}, dimensions={0} | all-to-all | bytes 294912 | tf_op jit(solution)/shard_map/all_to_all | solution.py:280
  51.8 3.0 %second_product.1 = (f32[16,8,1,384]{3,2,1,0:T(1,128)S(1)}, f32[6,192]{1,0:T(8,128)S(1)}, f32[6,192]{1,0:T(8,128)S(1)}) custom-call(f32[32,3,1,384]{3,2,1,0:T(1,128)S(1)} %all_to_all.26.arrived_ref, f32[192,192]{1,0:T(8,128)S(1)} %get-tuple-element.12.matrix_ref, f32[6,192]{1,0:T(8,128)S(1)} %get-tuple-element.13.residual_ref, ...), custom_call_target="tpu_custom_call" | custom-call | tf_op jit(solution)/shard_map/second_product/pallas_call | solution.py:324
  54.8 10.4 %all_to_all.27.arrived_ref = f32[16,8,1,384]{3,2,1,0:T(1,128)S(1)} all-to-all(f32[16,8,1,384]{3,2,1,0:T(1,128)S(1)} %get-tuple-element.15), channel_id=1, replica_groups=mesh['x'=4,'zh'=8,'zl'=2,'c'=2,'y'=4] {'x','zl','c'}, dimensions={0} | all-to-all | bytes 393216 | tf_op jit(solution)/shard_map/all_to_all | solution.py:280
  65.3 0.1 share.1
  65.4 16.1 %all_to_all.28.far_ref = f32[8,8,1,384]{3,2,1,0:T(1,128)S(1)} all-to-all(f32[8,8,1,384]{3,2,1,0:T(1,128)S(1)} %share.1), channel_id=1, replica_groups=mesh['x'=4,'zh'=8,'zl'=2,'c'=2,'y'=4] {'zh'}, dimensions={0} | all-to-all | bytes 196608 | tf_op jit(solution)/shard_map/all_to_all | solution.py:280
  81.5 0.2 dots.1
  81.7 15.2 %all_to_all.29.arrived_ref = f32[64,1,512]{2,1,0:T(1,128)S(1)} all-to-all(f32[64,1,512]{2,1,0:T(1,128)S(1)} %dots.1), channel_id=1, replica_groups=mesh['x'=4,'zh'=8,'zl'=2,'c'=2,'y'=4] {'x','zl','c','y'}, dimensions={0} | all-to-all | bytes 262144 | tf_op jit(solution)/shard_map/all_to_all | solution.py:280
  96.8 0.8 update.1

commit v8 on v7

--- a/solution.py
+++ b/solution.py
@@ -33,10 +33,6 @@
     return lax.broadcasted_iota(jnp.int32, shape, dim)
 
 
-def nt(a, b):
-    return lax.dot_general(a, b, (((1,), (1,)), ((), ())), precision=highest, preferred_element_type=f32)
-
-
 def split(value):
     high = value.astype(bf16)
     left = value - high.astype(f32)
@@ -46,6 +42,20 @@
 
 def one_pass(a, b):
     return jnp.dot(a, b, preferred_element_type=f32)
+
+
+def nt(vector, matrix):
+    padded = jnp.concatenate([vector, jnp.zeros((8 - SYS, UNK), f32)], axis=0)
+    rows = jnp.concatenate([p.astype(f32) for p in split(padded)], axis=0).astype(bf16)
+    total = None
+    for k, part in reversed(list(enumerate(split(matrix)))):
+        out = lax.dot_general(
+            rows[: 8 * (TILES - k)], part, (((1,), (1,)), ((), ())), preferred_element_type=f32
+        )
+        for e in reversed(range(TILES - k)):
+            piece = out[8 * e : 8 * e + 8]
+            total = piece if total is None else total + piece
+    return total[:SYS]
 
 
 def preconditioner(len_ref, inverse):
@@ -67,9 +77,12 @@
         last = jnp.where(inside, end, last)
         start = end
     pick = (iota((UNK, slots), 0) == target).astype(f32).astype(bf16)
-    rows = sum(one_pass(pick, part) for part in split(inverse))
-    spread = (iota((BLOCKS, UNK), 0) == column - first).astype(f32).astype(bf16)
-    full = sum(one_pass(part, spread) for part in split(rows))
+    parts = jnp.concatenate([p.astype(f32) for p in split(inverse)], axis=1).astype(bf16)
+    wide = one_pass(pick, parts)
+    fold = iota((TILES * BLOCKS, UNK), 0)
+    fold = fold - BLOCKS * ((fold >= BLOCKS).astype(jnp.int32) + (fold >= 2 * BLOCKS).astype(jnp.int32))
+    spread = (fold == column - first).astype(f32).astype(bf16)
+    full = one_pass(wide.astype(bf16), spread)
     row = iota((UNK, UNK), 0)
     return jnp.where((row >= first) & (row < last), full, 0.0)
 
@@ -212,10 +225,11 @@
 def share_kernel(arrived_ref, sent_ref):
     near = jnp.sum(arrived_ref[:, :EACH], axis=0)
     own = (lax.axis_index("y") * NL + lax.axis_index("zl")) * NC + lax.axis_index("c")
-    extra = arrived_ref[own, EACH:]
+    rows = [near[j] for j in range(EACH)] + [arrived_ref[own, EACH], arrived_ref[own, EACH + 1]]
     for k in range(NH):
-        sent_ref[k, :EACH] = near
-        sent_ref[k, EACH:] = extra
+        for j, row in enumerate(rows):
+            for i in range(TILES):
+                sent_ref[k, j * TILES + i : j * TILES + i + 1, :] = row[:, i * LANE : (i + 1) * LANE]
 
 
 def dots_kernel(far_ref, sent_ref):
@@ -224,13 +238,19 @@
     step = lax.axis_index("zh")
     mine = jnp.zeros((1, WIDE), f32)
     terms = [jnp.zeros((1, WIDE), f32)] * (2 * DOTS)
+    total = far_ref[0]
+    for k in range(1, NH):
+        total = total + far_ref[k]
+
+    def row(block, j):
+        return jnp.concatenate([block[j * TILES + i : j * TILES + i + 1] for i in range(TILES)], axis=1)
+
     for j in range(EACH):
-        t = far_ref[0, j]
-        for k in range(1, NH):
-            t = t + far_ref[k, j]
+        t = row(total, j)
         h = lax.rem(base + j, NH)
         mine = jnp.where(h == step, t, mine)
-        m, r = far_ref[h, EACH], far_ref[h, EACH + 1]
+        source = far_ref[h]
+        m, r = row(source, EACH), row(source, EACH + 1)
         same = lax.div(base + j, NH) == first
         for d, term in enumerate((r * r, r * m, m * m, t * r, t * m, t * t)):
             terms[d] = terms[d] + jnp.where(same, term, 0.0)
@@ -246,9 +266,9 @@
     shape = (2 * PAIR * DOTS, LANE)
     place = iota(shape, 0) + first * (PAIR * DOTS)
     line = jnp.sum(jnp.where(place == iota(shape, 1), column, 0.0), axis=0, keepdims=True)
-    row = jnp.concatenate([mine, line], axis=1)
+    sent = jnp.concatenate([mine, line], axis=1)
     for k in range(sent_ref.shape[0]):
-        sent_ref[k] = row
+        sent_ref[k] = sent
 
 
 def last_kernel(arrived_ref, iterate_ref, residual_ref, mapped_ref, lifted_ref, lifted_two_ref, new_iterate_ref, new_residual_ref):
@@ -331,7 +351,7 @@
         name="second_product",
     )(arrived, matrix, residual, held)
 
-    sent = call(share_kernel, "share", shape(NH, EACH + 2, 1, WIDE), exchanged(cut, ("x", "zl", "c")))
+    sent = call(share_kernel, "share", shape(NH, (EACH + 2) * TILES, LANE), exchanged(cut, ("x", "zl", "c")))
     sent = call(dots_kernel, "dots", shape(NX * NL * NC * NY, 1, WIDE + LANE), exchanged(sent, "zh"))
     arrived = exchanged(sent, ("x", "zl", "c", "y"))
     return call(last_kernel, "update", (small, small), arrived, iterate, residual, mapped, lifted, lifted_two)

time: 97.9 us -> 97.6 us (level)
  no operation moved by 1% of the time
where the time goes in v8:
time: 97.6 us; the launch traced here: 97.3 us
  blocking collectives  88 us (90%)
  Pallas kernels  8.66 us (9%)
    all_to_all x5, blocking collectives, exchanged(): return lax.all_to_all(pieces, axes, split_axis=0, concat_axis=0, tiled=True)  88 us
    pallas_call x1, Pallas kernels, body(): pl.pallas_call(first_kernel, out_shape=(shape(NZ, NC * PAIRS, 1, WIDE), s...  4.46 us
    pallas_call x1, Pallas kernels, body(): pl.pallas_call(second_kernel, out_shape=(shape(NX * NL * NC, EACH + 2, 1,...  2.98 us

profile of v8, /device:TPU:1, one launch (start us, length us, event | category | flops | bytes accessed | tf_op | source)
XLA Modules:
  0.0 97.3 jit_solution(1878590997688646557)
XLA Ops:
  0.6 4.5 %first_product.1 = (f32[16,6,1,384]{3,2,1,0:T(1,128)S(1)}, f32[192,192]{1,0:T(8,128)S(1)}, f32[6,192]{1,0:T(8,128)S(1)}, f32[6,192]{1,0:T(8,128)S(1)}, f32[6,192]{1,0:T(8,128)S(1)}, /*index=5*/f32[192,6144]{1,0:T(8,128)S(1)}) custom-call(s32[1,24]{1,0:T(1,128)} %len_hbm.1, f32[576,24]{1,0:T(8,128)} %bitcast.1, f32[6,192]{1,0:T(8,128)} %residual_hbm.1, ...), custom_call_target="tpu_custom_call" | custom-call | tf_op jit(solution)/shard_map/first_product/pallas_call | solution.py:315
  5.1 27.6 %all_to_all.25.arrived_ref = f32[16,6,1,384]{3,2,1,0:T(1,128)S(1)} all-to-all(f32[16,6,1,384]{3,2,1,0:T(1,128)S(1)} %get-tuple-element.11), channel_id=1, replica_groups=mesh['x'=4,'zh'=8,'zl'=2,'c'=2,'y'=4] {'zh','zl'}, dimensions={0} | all-to-all | bytes 294912 | tf_op jit(solution)/shard_map/all_to_all | solution.py:300
  32.7 0.1 forward.1
  32.8 18.6 %all_to_all.26.arrived_ref = f32[32,3,1,384]{3,2,1,0:T(1,128)S(1)} all-to-all(f32[32,3,1,384]{3,2,1,0:T(1,128)S(1)} %forward.1), channel_id=1, replica_groups=mesh['x'=4,'zh'=8,'zl'=2,'c'=2,'y'=4] {'x','c','y'}, dimensions={0} | all-to-all | bytes 294912 | tf_op jit(solution)/shard_map/all_to_all | solution.py:300
  51.4 3.0 %second_product.1 = (f32[16,8,1,384]{3,2,1,0:T(1,128)S(1)}, f32[6,192]{1,0:T(8,128)S(1)}, f32[6,192]{1,0:T(8,128)S(1)}) custom-call(f32[32,3,1,384]{3,2,1,0:T(1,128)S(1)} %all_to_all.26.arrived_ref, f32[192,192]{1,0:T(8,128)S(1)} %get-tuple-element.12.matrix_ref, f32[6,192]{1,0:T(8,128)S(1)} %get-tuple-element.13.residual_ref, ...), custom_call_target="tpu_custom_call" | custom-call | tf_op jit(solution)/shard_map/second_product/pallas_call | solution.py:344
  54.4 10.4 %all_to_all.27.arrived_ref = f32[16,8,1,384]{3,2,1,0:T(1,128)S(1)} all-to-all(f32[16,8,1,384]{3,2,1,0:T(1,128)S(1)} %get-tuple-element.15), channel_id=1, replica_groups=mesh['x'=4,'zh'=8,'zl'=2,'c'=2,'y'=4] {'x','zl','c'}, dimensions={0} | all-to-all | bytes 393216 | tf_op jit(solution)/shard_map/all_to_all | solution.py:300
  64.9 0.1 share.1
  65.0 16.1 %all_to_all.28.far_ref = f32[8,24,128]{2,1,0:T(8,128)S(1)} all-to-all(f32[8,24,128]{2,1,0:T(8,128)S(1)} %share.1), channel_id=1, replica_groups=mesh['x'=4,'zh'=8,'zl'=2,'c'=2,'y'=4] {'zh'}, dimensions={0} | all-to-all | bytes 196608 | tf_op jit(solution)/shard_map/all_to_all | solution.py:300
  81.1 0.2 dots.1
  81.3 15.2 %all_to_all.29.arrived_ref = f32[64,1,512]{2,1,0:T(1,128)S(1)} all-to-all(f32[64,1,512]{2,1,0:T(1,128)S(1)} %dots.1), channel_id=1, replica_groups=mesh['x'=4,'zh'=8,'zl'=2,'c'=2,'y'=4] {'x','zl','c','y'}, dimensions={0} | all-to-all | bytes 262144 | tf_op jit(solution)/shard_map/all_to_all | solution.py:300
  96.5 0.8 update.1

commit v9 on v8

--- a/solution.py
+++ b/solution.py
@@ -202,11 +202,12 @@
         total = part if total is None else total + part
     mapped = decoded([total[p] for p in range(PAIRS)], core)
     matrix = matrix_ref[...]
+    far = lax.div(lax.axis_index("zh"), NH // 2)
 
     def home(p, z, c):
         row = p * NH + lax.div(z, NL)
         x = lax.div(row, EACH)
-        return (x * NL + lax.rem(z, NL)) * NC + c, row - x * EACH
+        return (x * NL + lax.rem(z, NL)) * NC + lax.rem(c + far, NC), row - x * EACH
 
     product(matrix, mapped, lifted_ref, None, held, spread, cut_ref, home)
     step = lax.axis_index("zh")
@@ -224,7 +225,7 @@
 
 def share_kernel(arrived_ref, sent_ref):
     near = jnp.sum(arrived_ref[:, :EACH], axis=0)
-    own = (lax.axis_index("y") * NL + lax.axis_index("zl")) * NC + lax.axis_index("c")
+    own = (lax.axis_index("y") * NL + lax.axis_index("zl")) * NC + turned_core()
     rows = [near[j] for j in range(EACH)] + [arrived_ref[own, EACH], arrived_ref[own, EACH + 1]]
     for k in range(NH):
         for j, row in enumerate(rows):
@@ -288,7 +289,7 @@
     rows = []
     for p in range(PAIRS):
         source = lax.div(p * NH + lax.axis_index("zh"), EACH)
-        rows.append(arrived_ref[((source * NL + lax.axis_index("zl")) * NC + core) * NY + x][:, :WIDE])
+        rows.append(arrived_ref[((source * NL + lax.axis_index("zl")) * NC + turned_core()) * NY + x][:, :WIDE])
     mapped_two = decoded(rows, core)
     middle = residual_ref[...] - alpha * mapped
     lifted_mid = lifted - alpha * lifted_two_ref[...]
@@ -296,8 +297,16 @@
     new_residual_ref[...] = middle - omega * (mapped - alpha * mapped_two)
 
 
-def exchanged(pieces, axes):
-    return lax.all_to_all(pieces, axes, split_axis=0, concat_axis=0, tiled=True)
+def exchanged(pieces, axes, groups=None):
+    return lax.all_to_all(pieces, axes, split_axis=0, concat_axis=0, tiled=True, axis_index_groups=groups)
+
+
+def crossed(length):
+    return [[k * NC + (g + 2 * k // length) % NC for k in range(length)] for g in range(NC)]
+
+
+def turned_core():
+    return lax.rem(lax.axis_index("c") + lax.div(lax.axis_index("zh"), NH // 2), NC)
 
 
 def body(operator, block_inverse, block_len, iterate, residual):
@@ -338,7 +347,7 @@
             name=name,
         )(*operands)
 
-    sent = call(forward_kernel, "forward", shape(NX * NC * NY, PAIRS, 1, WIDE), exchanged(cut, Z))
+    sent = call(forward_kernel, "forward", shape(NX * NC * NY, PAIRS, 1, WIDE), exchanged(cut, (*Z, "c"), crossed(NZ)))
     arrived = exchanged(sent, ("x", "c", "y"))
 
     cut, mapped, lifted_two = pl.pallas_call(
@@ -352,7 +361,7 @@
     )(arrived, matrix, residual, held)
 
     sent = call(share_kernel, "share", shape(NH, (EACH + 2) * TILES, LANE), exchanged(cut, ("x", "zl", "c")))
-    sent = call(dots_kernel, "dots", shape(NX * NL * NC * NY, 1, WIDE + LANE), exchanged(sent, "zh"))
+    sent = call(dots_kernel, "dots", shape(NX * NL * NC * NY, 1, WIDE + LANE), exchanged(sent, ("zh", "c"), crossed(NH)))
     arrived = exchanged(sent, ("x", "zl", "c", "y"))
     return call(last_kernel, "update", (small, small), arrived, iterate, residual, mapped, lifted, lifted_two)
 

time: 97.6 us -> 97.6 us (level)
  no operation moved by 1% of the time
where the time goes in v9:
time: 97.6 us; the launch traced here: 97.3 us
  blocking collectives  88 us (90%)
  Pallas kernels  8.66 us (9%)
    all_to_all x5, blocking collectives, exchanged(): lax.all_to_all(pieces, axes, split_axis=0, concat_axis=0, tiled=True, axi...  88 us
    pallas_call x1, Pallas kernels, body(): pl.pallas_call(first_kernel, out_shape=(shape(NZ, NC * PAIRS, 1, WIDE), s...  4.46 us
    pallas_call x1, Pallas kernels, body(): pl.pallas_call(second_kernel, out_shape=(shape(NX * NL * NC, EACH + 2, 1,...  2.98 us

profile of v9, /device:TPU:1, one launch (start us, length us, event | category | flops | bytes accessed | tf_op | source)
XLA Modules:
  0.0 97.3 jit_solution(4476732175195166970)
XLA Ops:
  0.6 4.5 %first_product.1 = (f32[16,6,1,384]{3,2,1,0:T(1,128)S(1)}, f32[192,192]{1,0:T(8,128)S(1)}, f32[6,192]{1,0:T(8,128)S(1)}, f32[6,192]{1,0:T(8,128)S(1)}, f32[6,192]{1,0:T(8,128)S(1)}, /*index=5*/f32[192,6144]{1,0:T(8,128)S(1)}) custom-call(s32[1,24]{1,0:T(1,128)} %len_hbm.1, f32[576,24]{1,0:T(8,128)} %bitcast.1, f32[6,192]{1,0:T(8,128)} %residual_hbm.1, ...), custom_call_target="tpu_custom_call" | custom-call | tf_op jit(solution)/shard_map/first_product/pallas_call | solution.py:324
  5.1 30.1 %all_to_all.25.arrived_ref = f32[16,6,1,384]{3,2,1,0:T(1,128)S(1)} all-to-all(f32[16,6,1,384]{3,2,1,0:T(1,128)S(1)} %get-tuple-element.11), channel_id=1, replica_groups={{0,8,16,24,32,40,48,56,68,76,84,92,100,108,116,124},{4,12,20,28,36,44,5..., dimensions={0} | all-to-all | bytes 294912 | tf_op jit(solution)/shard_map/all_to_all | solution.py:301
  35.1 0.1 forward.1
  35.3 14.7 %all_to_all.26.arrived_ref = f32[32,3,1,384]{3,2,1,0:T(1,128)S(1)} all-to-all(f32[32,3,1,384]{3,2,1,0:T(1,128)S(1)} %forward.1), channel_id=1, replica_groups=mesh['x'=4,'zh'=8,'zl'=2,'c'=2,'y'=4] {'x','c','y'}, dimensions={0} | all-to-all | bytes 294912 | tf_op jit(solution)/shard_map/all_to_all | solution.py:301
  50.0 3.0 %second_product.1 = (f32[16,8,1,384]{3,2,1,0:T(1,128)S(1)}, f32[6,192]{1,0:T(8,128)S(1)}, f32[6,192]{1,0:T(8,128)S(1)}) custom-call(f32[32,3,1,384]{3,2,1,0:T(1,128)S(1)} %all_to_all.26.arrived_ref, f32[192,192]{1,0:T(8,128)S(1)} %get-tuple-element.12.matrix_ref, f32[6,192]{1,0:T(8,128)S(1)} %get-tuple-element.13.residual_ref, ...), custom_call_target="tpu_custom_call" | custom-call | tf_op jit(solution)/shard_map/second_product/pallas_call | solution.py:353
  53.0 11.9 %all_to_all.27.arrived_ref = f32[16,8,1,384]{3,2,1,0:T(1,128)S(1)} all-to-all(f32[16,8,1,384]{3,2,1,0:T(1,128)S(1)} %get-tuple-element.15), channel_id=1, replica_groups=mesh['x'=4,'zh'=8,'zl'=2,'c'=2,'y'=4] {'x','zl','c'}, dimensions={0} | all-to-all | bytes 393216 | tf_op jit(solution)/shard_map/all_to_all | solution.py:301
  64.9 0.1 share.1
  65.0 18.8 %all_to_all.28.far_ref = f32[8,24,128]{2,1,0:T(8,128)S(1)} all-to-all(f32[8,24,128]{2,1,0:T(8,128)S(1)} %share.1), channel_id=1, replica_groups={{0,16,32,48,68,84,100,116},{4,20,36,52,64,80,96,112},{1,17,33,49,69,85,..., dimensions={0} | all-to-all | bytes 196608 | tf_op jit(solution)/shard_map/all_to_all | solution.py:301
  83.8 0.2 dots.1
  84.0 12.5 %all_to_all.29.arrived_ref = f32[64,1,512]{2,1,0:T(1,128)S(1)} all-to-all(f32[64,1,512]{2,1,0:T(1,128)S(1)} %dots.1), channel_id=1, replica_groups=mesh['x'=4,'zh'=8,'zl'=2,'c'=2,'y'=4] {'x','zl','c','y'}, dimensions={0} | all-to-all | bytes 262144 | tf_op jit(solution)/shard_map/all_to_all | solution.py:301
  96.5 0.8 update.1

commit v10 on v9

--- a/solution.py
+++ b/solution.py
@@ -347,7 +347,7 @@
             name=name,
         )(*operands)
 
-    sent = call(forward_kernel, "forward", shape(NX * NC * NY, PAIRS, 1, WIDE), exchanged(cut, (*Z, "c"), crossed(NZ)))
+    sent = call(forward_kernel, "forward", shape(NX * NC * NY, PAIRS, 1, WIDE), exchanged(cut, Z))
     arrived = exchanged(sent, ("x", "c", "y"))
 
     cut, mapped, lifted_two = pl.pallas_call(

time: 97.6 us -> 97 us (level)
  no operation moved by 1% of the time
where the time goes in v10:
time: 97 us; the launch traced here: 96.7 us
  blocking collectives  87.4 us (90%)
  Pallas kernels  8.66 us (9%)
    all_to_all x5, blocking collectives, exchanged(): lax.all_to_all(pieces, axes, split_axis=0, concat_axis=0, tiled=True, axi...  87.4 us
    pallas_call x1, Pallas kernels, body(): pl.pallas_call(first_kernel, out_shape=(shape(NZ, NC * PAIRS, 1, WIDE), s...  4.46 us
    pallas_call x1, Pallas kernels, body(): pl.pallas_call(second_kernel, out_shape=(shape(NX * NL * NC, EACH + 2, 1,...  2.98 us

profile of v10, /device:TPU:1, one launch (start us, length us, event | category | flops | bytes accessed | tf_op | source)
XLA Modules:
  0.0 96.7 jit_solution(10095883520708656326)
XLA Ops:
  0.6 4.5 %first_product.1 = (f32[16,6,1,384]{3,2,1,0:T(1,128)S(1)}, f32[192,192]{1,0:T(8,128)S(1)}, f32[6,192]{1,0:T(8,128)S(1)}, f32[6,192]{1,0:T(8,128)S(1)}, f32[6,192]{1,0:T(8,128)S(1)}, /*index=5*/f32[192,6144]{1,0:T(8,128)S(1)}) custom-call(s32[1,24]{1,0:T(1,128)} %len_hbm.1, f32[576,24]{1,0:T(8,128)} %bitcast.1, f32[6,192]{1,0:T(8,128)} %residual_hbm.1, ...), custom_call_target="tpu_custom_call" | custom-call | tf_op jit(solution)/shard_map/first_product/pallas_call | solution.py:324
  5.1 27.6 %all_to_all.25.arrived_ref = f32[16,6,1,384]{3,2,1,0:T(1,128)S(1)} all-to-all(f32[16,6,1,384]{3,2,1,0:T(1,128)S(1)} %get-tuple-element.11), channel_id=1, replica_groups=mesh['x'=4,'zh'=8,'zl'=2,'c'=2,'y'=4] {'zh','zl'}, dimensions={0} | all-to-all | bytes 294912 | tf_op jit(solution)/shard_map/all_to_all | solution.py:301
  32.7 0.1 forward.1
  32.8 18.6 %all_to_all.26.arrived_ref = f32[32,3,1,384]{3,2,1,0:T(1,128)S(1)} all-to-all(f32[32,3,1,384]{3,2,1,0:T(1,128)S(1)} %forward.1), channel_id=1, replica_groups=mesh['x'=4,'zh'=8,'zl'=2,'c'=2,'y'=4] {'x','c','y'}, dimensions={0} | all-to-all | bytes 294912 | tf_op jit(solution)/shard_map/all_to_all | solution.py:301
  51.4 3.0 %second_product.1 = (f32[16,8,1,384]{3,2,1,0:T(1,128)S(1)}, f32[6,192]{1,0:T(8,128)S(1)}, f32[6,192]{1,0:T(8,128)S(1)}) custom-call(f32[32,3,1,384]{3,2,1,0:T(1,128)S(1)} %all_to_all.26.arrived_ref, f32[192,192]{1,0:T(8,128)S(1)} %get-tuple-element.12.matrix_ref, f32[6,192]{1,0:T(8,128)S(1)} %get-tuple-element.13.residual_ref, ...), custom_call_target="tpu_custom_call" | custom-call | tf_op jit(solution)/shard_map/second_product/pallas_call | solution.py:353
  54.4 10.4 %all_to_all.27.arrived_ref = f32[16,8,1,384]{3,2,1,0:T(1,128)S(1)} all-to-all(f32[16,8,1,384]{3,2,1,0:T(1,128)S(1)} %get-tuple-element.15), channel_id=1, replica_groups=mesh['x'=4,'zh'=8,'zl'=2,'c'=2,'y'=4] {'x','zl','c'}, dimensions={0} | all-to-all | bytes 393216 | tf_op jit(solution)/shard_map/all_to_all | solution.py:301
  64.9 0.1 share.1
  65.0 18.3 %all_to_all.28.far_ref = f32[8,24,128]{2,1,0:T(8,128)S(1)} all-to-all(f32[8,24,128]{2,1,0:T(8,128)S(1)} %share.1), channel_id=1, replica_groups={{0,16,32,48,68,84,100,116},{4,20,36,52,64,80,96,112},{1,17,33,49,69,85,..., dimensions={0} | all-to-all | bytes 196608 | tf_op jit(solution)/shard_map/all_to_all | solution.py:301
  83.3 0.2 dots.1
  83.5 12.5 %all_to_all.29.arrived_ref = f32[64,1,512]{2,1,0:T(1,128)S(1)} all-to-all(f32[64,1,512]{2,1,0:T(1,128)S(1)} %dots.1), channel_id=1, replica_groups=mesh['x'=4,'zh'=8,'zl'=2,'c'=2,'y'=4] {'x','zl','c','y'}, dimensions={0} | all-to-all | bytes 262144 | tf_op jit(solution)/shard_map/all_to_all | solution.py:301
  96.0 0.8 update.1

commit v11 on v10

--- a/solution.py
+++ b/solution.py
@@ -250,8 +250,10 @@
         t = row(total, j)
         h = lax.rem(base + j, NH)
         mine = jnp.where(h == step, t, mine)
-        source = far_ref[h]
-        m, r = row(source, EACH), row(source, EACH + 1)
+        m, r = (
+            jnp.concatenate([far_ref[h, k * TILES + i : k * TILES + i + 1, :] for i in range(TILES)], axis=1)
+            for k in (EACH, EACH + 1)
+        )
         same = lax.div(base + j, NH) == first
         for d, term in enumerate((r * r, r * m, m * m, t * r, t * m, t * t)):
             terms[d] = terms[d] + jnp.where(same, term, 0.0)

time: 97 us -> 97 us (level)
  no operation moved by 1% of the time
where the time goes in v11:
time: 97 us; the launch traced here: 96.8 us
  blocking collectives  87.4 us (90%)
  Pallas kernels  8.67 us (9%)
    all_to_all x5, blocking collectives, exchanged(): lax.all_to_all(pieces, axes, split_axis=0, concat_axis=0, tiled=True, axi...  87.4 us
    pallas_call x1, Pallas kernels, body(): pl.pallas_call(first_kernel, out_shape=(shape(NZ, NC * PAIRS, 1, WIDE), s...  4.46 us
    pallas_call x1, Pallas kernels, body(): pl.pallas_call(second_kernel, out_shape=(shape(NX * NL * NC, EACH + 2, 1,...  2.98 us

profile of v11, /device:TPU:1, one launch (start us, length us, event | category | flops | bytes accessed | tf_op | source)
XLA Modules:
  0.0 96.8 jit_solution(4422557349793447096)
XLA Ops:
  0.6 4.5 %first_product.1 = (f32[16,6,1,384]{3,2,1,0:T(1,128)S(1)}, f32[192,192]{1,0:T(8,128)S(1)}, f32[6,192]{1,0:T(8,128)S(1)}, f32[6,192]{1,0:T(8,128)S(1)}, f32[6,192]{1,0:T(8,128)S(1)}, /*index=5*/f32[192,6144]{1,0:T(8,128)S(1)}) custom-call(s32[1,24]{1,0:T(1,128)} %len_hbm.1, f32[576,24]{1,0:T(8,128)} %bitcast.1, f32[6,192]{1,0:T(8,128)} %residual_hbm.1, ...), custom_call_target="tpu_custom_call" | custom-call | tf_op jit(solution)/shard_map/first_product/pallas_call | solution.py:326
  5.1 27.6 %all_to_all.25.arrived_ref = f32[16,6,1,384]{3,2,1,0:T(1,128)S(1)} all-to-all(f32[16,6,1,384]{3,2,1,0:T(1,128)S(1)} %get-tuple-element.11), channel_id=1, replica_groups=mesh['x'=4,'zh'=8,'zl'=2,'c'=2,'y'=4] {'zh','zl'}, dimensions={0} | all-to-all | bytes 294912 | tf_op jit(solution)/shard_map/all_to_all | solution.py:303
  32.7 0.1 forward.1
  32.8 18.6 %all_to_all.26.arrived_ref = f32[32,3,1,384]{3,2,1,0:T(1,128)S(1)} all-to-all(f32[32,3,1,384]{3,2,1,0:T(1,128)S(1)} %forward.1), channel_id=1, replica_groups=mesh['x'=4,'zh'=8,'zl'=2,'c'=2,'y'=4] {'x','c','y'}, dimensions={0} | all-to-all | bytes 294912 | tf_op jit(solution)/shard_map/all_to_all | solution.py:303
  51.4 3.0 %second_product.1 = (f32[16,8,1,384]{3,2,1,0:T(1,128)S(1)}, f32[6,192]{1,0:T(8,128)S(1)}, f32[6,192]{1,0:T(8,128)S(1)}) custom-call(f32[32,3,1,384]{3,2,1,0:T(1,128)S(1)} %all_to_all.26.arrived_ref, f32[192,192]{1,0:T(8,128)S(1)} %get-tuple-element.12.matrix_ref, f32[6,192]{1,0:T(8,128)S(1)} %get-tuple-element.13.residual_ref, ...), custom_call_target="tpu_custom_call" | custom-call | tf_op jit(solution)/shard_map/second_product/pallas_call | solution.py:355
  54.4 10.4 %all_to_all.27.arrived_ref = f32[16,8,1,384]{3,2,1,0:T(1,128)S(1)} all-to-all(f32[16,8,1,384]{3,2,1,0:T(1,128)S(1)} %get-tuple-element.15), channel_id=1, replica_groups=mesh['x'=4,'zh'=8,'zl'=2,'c'=2,'y'=4] {'x','zl','c'}, dimensions={0} | all-to-all | bytes 393216 | tf_op jit(solution)/shard_map/all_to_all | solution.py:303
  64.9 0.1 share.1
  65.0 18.3 %all_to_all.28.far_ref = f32[8,24,128]{2,1,0:T(8,128)S(1)} all-to-all(f32[8,24,128]{2,1,0:T(8,128)S(1)} %share.1), channel_id=1, replica_groups={{0,16,32,48,68,84,100,116},{4,20,36,52,64,80,96,112},{1,17,33,49,69,85,..., dimensions={0} | all-to-all | bytes 196608 | tf_op jit(solution)/shard_map/all_to_all | solution.py:303
  83.3 0.2 dots.1
  83.5 12.5 %all_to_all.29.arrived_ref = f32[64,1,512]{2,1,0:T(1,128)S(1)} all-to-all(f32[64,1,512]{2,1,0:T(1,128)S(1)} %dots.1), channel_id=1, replica_groups=mesh['x'=4,'zh'=8,'zl'=2,'c'=2,'y'=4] {'x','zl','c','y'}, dimensions={0} | all-to-all | bytes 262144 | tf_op jit(solution)/shard_map/all_to_all | solution.py:303
  96.0 0.8 update.1
